TPU v7x, 256 devices: a whole 4x4x8 slice. The times are simulated.
256 devices in a mesh: seq: 32 (over y, x, core), head: 8 (over z).
Axes of the slice: x: 4, y: 4, z: 8, core: 2. Of those that a mesh axis runs over, the one named last changes fastest.
Arguments:
- inputs: bfloat16 [8192, 4096], P('seq', 'head'), may hold values from -6 to 6
- gates: bfloat16 [8192, 4096], P('seq', 'head'), may hold values from -6 to 6
- b_proj: bfloat16 [8192, 128], P('seq'), may hold values from -6 to 6
- c_proj: bfloat16 [8192, 128], P('seq'), may hold values from -6 to 6
- step_size: float32 [64, 8192], P('head', 'seq'), may hold values from 0 to 2
- decay_rate: float32 [64], P('head'), may hold values from 0.5 to 2
- norm_gain: float32 [4096], P('head'), may hold values from 0.5 to 1.5
- out_weight: bfloat16 [4096, 4096], P('seq', 'head'), may hold values from -0.09375 to 0.09375
- grad_out: bfloat16 [8192, 4096], P('seq', 'head'), may hold values from -6 to 6
Outputs:
- grad_inputs: bfloat16 [8192, 4096], P('seq', 'head')
- grad_gates: bfloat16 [8192, 4096], P('seq', 'head')
- grad_b: float32 [8192, 128], P('seq')
- grad_c: float32 [8192, 128], P('seq')
- grad_step: float32 [64, 8192], P('head', 'seq')
- grad_rate: float32 [64], P('head')
- grad_gain: float32 [4096], P('head')
- grad_weight: float32 [4096, 4096], P('seq', 'head')
All inputs are finite; a program needn't handle non-finite values.
Results may differ from a plain program's by a relative error of at most 0.0042.
Values may be sent and summed in bfloat16 or wider, within the bound.
A program may use at most 64 MiB of HBM per device.

v0:
```python
import jax
import jax.numpy as jnp
from jax import lax
from jax.sharding import Mesh
from jax.sharding import PartitionSpec as P

SEQ = ("seq_0", "seq_1", "seq_2")


EPSILON = 1e-05


def joined_along(tiles, dim):
    dims = list(tiles.shape[1:])
    dims[dim] *= tiles.shape[0]
    return jnp.moveaxis(tiles, 0, dim).reshape(dims)


def copy_for_each(x, axis):
    peers = lax.axis_size(axis)
    return lax.all_to_all(jnp.broadcast_to(x[None], (peers, *x.shape)), axis, 0, 0, tiled=True)


def gathered_copies(x, axis, dim):
    return joined_along(copy_for_each(x, axis), dim)


def nothing_yet(x, identity):
    return jax.tree.map(
        lambda part, zero: jnp.zeros_like(part) + jnp.asarray(zero, part.dtype), x, identity
    )


def entering(x, axes, combine, identity, reverse):
    before = start = nothing_yet(x, identity)
    so_far = x
    for axis in reversed(axes):
        peers, position = (lax.axis_size(axis), lax.axis_index(axis))
        pieces = jax.tree.map(lambda part: lax.all_gather(part, axis), so_far)
        inside, so_far = (start, start)
        for k in reversed(range(peers)) if reverse else range(peers):
            passed = k > position if reverse else k < position
            so_far = combine(so_far, jax.tree.map(lambda part: part[k], pieces))
            inside = jax.tree.map(lambda new, old: jnp.where(passed, new, old), so_far, inside)
        before = combine(inside, before)
    return before


def taken_together(x, axis):
    everything = copy_for_each(x, axis)
    return jnp.sum(everything, axis=0)


def packed_total(arrays, axis):
    ends = [0]
    for a in arrays:
        ends.append(ends[-1] + a.size)
    so_far = taken_together(jnp.concatenate([a.ravel() for a in arrays]), axis)
    return tuple((so_far[b:e].reshape(a.shape) for a, b, e in zip(arrays, ends, ends[1:])))


def dot_high(left, right):
    return jnp.dot(left, right, precision=lax.Precision.HIGHEST, preferred_element_type=jnp.float32)


def dot_inner(left, right):
    return lax.dot_general(
        left,
        right,
        (((0,), (0,)), ((), ())),
        precision=lax.Precision.HIGHEST,
        preferred_element_type=jnp.float32,
    )


def decay_table(step, rate):
    logs = -jnp.cumsum(rate * step)
    count = step.shape[0]
    later = lax.broadcasted_iota(jnp.int32, (count, count), 0)
    earlier = lax.broadcasted_iota(jnp.int32, (count, count), 1)
    spread = jnp.minimum(logs[:, None] - logs[None, :], 0.0)
    table = jnp.where(later >= earlier, jnp.exp(spread), 0.0)
    return (logs, table)


def span_summary(step, rate, values, keys_b):
    logs = -jnp.cumsum(rate * step)
    tail = jnp.exp(logs[-1] - logs)
    return (jnp.exp(logs[-1]), dot_inner(keys_b * (step * tail)[:, None], values))


def span_output(step, rate, values, keys_b, queries_c, state_in):
    logs, table = decay_table(step, rate)
    scores = dot_high(queries_c, keys_b.T)
    mixing = table * scores * step[None, :]
    return dot_high(mixing, values) + jnp.exp(logs)[:, None] * dot_high(queries_c, state_in)


def adjoint_summary(step, rate, queries_c, grads):
    logs = -jnp.cumsum(rate * step)
    return (jnp.exp(logs[-1]), dot_inner(queries_c * jnp.exp(logs)[:, None], grads))


def span_backward(step, rate, values, keys_b, queries_c, grads, state_in, adjoint_in):
    logs, table = decay_table(step, rate)
    tail = jnp.exp(logs[-1] - logs)
    front = jnp.exp(logs)
    scores = dot_high(queries_c, keys_b.T)
    inner = dot_high(grads, values.T)
    weighted = table * inner
    mixing = table * scores * step[None, :]
    keys_adjoint = dot_high(keys_b, adjoint_in)
    grad_values = dot_inner(mixing, grads) + (step * tail)[:, None] * keys_adjoint
    grad_keys = step[:, None] * (
        dot_inner(weighted, queries_c) + tail[:, None] * dot_high(values, adjoint_in.T)
    )
    grad_queries = dot_high(weighted * step[None, :], keys_b) + front[:, None] * dot_high(
        grads, state_in.T
    )
    carried = tail * jnp.sum(keys_adjoint * values, axis=1)
    q_terms = jnp.sum(weighted * scores, axis=0) + carried
    row_part = jnp.sum(mixing * inner, axis=1) + front * jnp.sum(
        dot_high(queries_c, state_in) * grads, axis=1
    )
    drive = row_part - step * q_terms
    state_end = jnp.exp(logs[-1]) * state_in + dot_inner(keys_b * (step * tail)[:, None], values)
    boundary = jnp.sum(adjoint_in * state_end)
    log_grad = jnp.flip(jnp.cumsum(jnp.flip(drive))) + boundary
    grad_step = q_terms - rate * log_grad
    rate_part = -jnp.sum(step * log_grad)
    return (grad_values, grad_keys, grad_queries, grad_step, rate_part)


def combine(earlier, later):
    return (earlier[0] * later[0], later[1] + later[0][:, None, None] * earlier[1])


def on_device(
    inputs, gates, b_proj, c_proj, step_size, decay_rate, norm_gain, out_weight, grad_out
):
    length, width = inputs.shape
    heads = step_size.shape[0]
    head_width = width // heads
    values = inputs.astype(jnp.float32).reshape(length, heads, head_width).transpose(1, 0, 2)
    keys_b = b_proj.astype(jnp.float32)
    queries_c = c_proj.astype(jnp.float32)
    grad_full = gathered_copies(grad_out, "head", 1)
    columns = grad_full
    grad_normed = jnp.dot(
        columns,
        lax.all_gather(out_weight, SEQ, axis=0, tiled=True),
        preferred_element_type=jnp.float32,
    )
    decays, local_states = jax.vmap(span_summary, in_axes=(0, 0, 0, None))(
        step_size, decay_rate, values, keys_b
    )
    identity = (jnp.ones_like(decays), jnp.zeros_like(local_states))
    _, state_in = entering((decays, local_states), SEQ, combine, identity, False)

    def output_head(items):
        step, rate, head_values, state = items
        return span_output(step, rate, head_values, keys_b, queries_c, state)

    head_out = lax.map(output_head, (step_size, decay_rate, values, state_in))
    ssd_out = head_out.transpose(1, 0, 2).reshape(length, width)
    gate_values = gates.astype(jnp.float32)
    sigmoid_gate = jax.nn.sigmoid(gate_values)
    gated = ssd_out * gate_values * sigmoid_gate
    total_width = width * lax.axis_size("head")
    scaled = grad_normed * norm_gain[None, :]
    squares, cross = packed_total(
        (jnp.sum(gated * gated, axis=1), jnp.sum(scaled * gated, axis=1)), "head"
    )
    inv_rms = lax.rsqrt(squares / total_width + EPSILON)
    normed = (gated * inv_rms[:, None] * norm_gain[None, :]).astype(jnp.bfloat16)
    gain_part = jnp.sum(grad_normed * gated * inv_rms[:, None], axis=0)
    grad_gated = inv_rms[:, None] * (
        scaled - gated * (inv_rms * inv_rms * cross / total_width)[:, None]
    )
    grad_ssd = grad_gated * gate_values * sigmoid_gate
    grad_gates = (
        grad_gated * ssd_out * sigmoid_gate * (1.0 + gate_values * (1.0 - sigmoid_gate))
    ).astype(jnp.bfloat16)
    grads = grad_ssd.reshape(length, heads, head_width).transpose(1, 0, 2)
    back_decays, back_local = jax.vmap(adjoint_summary, in_axes=(0, 0, None, 0))(
        step_size, decay_rate, queries_c, grads
    )
    _, adjoint_in = entering((back_decays, back_local), SEQ, combine, identity, True)

    def backward_head(items):
        step, rate, head_values, head_grads, state, adjoint = items
        return span_backward(step, rate, head_values, keys_b, queries_c, head_grads, state, adjoint)

    grad_values, grad_keys, grad_queries, grad_step, rate_part = lax.map(
        backward_head, (step_size, decay_rate, values, grads, state_in, adjoint_in)
    )
    grad_inputs = grad_values.transpose(1, 0, 2).reshape(length, width).astype(jnp.bfloat16)
    grad_b, grad_c = packed_total(
        (jnp.sum(grad_keys, axis=0), jnp.sum(grad_queries, axis=0)), "head"
    )
    grad_gain, grad_rate = (taken_together(gain_part, SEQ), taken_together(rate_part, SEQ))
    columns = grad_full
    grad_weight = lax.psum_scatter(
        lax.dot_general(
            columns, normed, (((0,), (0,)), ((), ())), preferred_element_type=jnp.float32
        ),
        SEQ,
        scatter_dimension=0,
        tiled=True,
    )
    return (grad_inputs, grad_gates, grad_b, grad_c, grad_step, grad_rate, grad_gain, grad_weight)


def solution(mesh):
    split = Mesh(
        mesh.devices.reshape(4, 4, 2, mesh.shape["head"]), ("seq_0", "seq_1", "seq_2", "head")
    )
    return jax.shard_map(
        on_device,
        mesh=split,
        in_specs=(
            P(SEQ, "head"),
            P(SEQ, "head"),
            P(SEQ, None),
            P(SEQ, None),
            P("head", SEQ),
            P("head"),
            P("head"),
            P(SEQ, "head"),
            P(SEQ, "head"),
        ),
        out_specs=(
            P(SEQ, "head"),
            P(SEQ, "head"),
            P(SEQ, None),
            P(SEQ, None),
            P("head", SEQ),
            P("head"),
            P("head"),
            P(SEQ, "head"),
        ),
        check_vma=False,
    )
```

profile of v0, /device:TPU:1, one launch (start us, length us, event | category | flops | bytes accessed | tf_op | source)
XLA Modules:
  0.0 464.2 jit_solution(2456860582595576139)
XLA Ops:
  12.6 5.0 %all-gather = f32[16,128,64]{1,2,0:T(8,128)S(1)} all-gather(f32[8,128,64]{1,2,0:T(8,128)S(1)} %fusion.76), channel_id=2, replica_groups=mesh['seq_0'=4,'seq_1'=4,'seq_2'=2,'head'=8] {'seq_2'}, dimensions={0}, use_global_device_ids=true | all-gather | bytes 786432 | tf_op jit(solution)/shard_map/all_gather | solution.py:39
  20.3 2.5 all-reduce
  22.9 6.7 %all-reduce.1 = f32[32]{0:T(128)S(1)} all-reduce(f32[32]{0:T(128)S(1)} %multiply_dynamic-update-slice_fusion), channel_id=5, replica_groups=mesh['seq_0'=4,'seq_1'=4,'seq_2'=2,'head'=8] {'seq_1'}, use_global_device_ids=true, to_apply=%add.1 | all-reduce | flops 32 | bytes 256
  31.9 26.4 %all-gather.12.cloned.1.call-done = f32[4,8,128,64]{2,3,1,0:T(8,128)} async-done(((f32[1,8,128,64]{2,3,1,0:T(8,128)}), f32[4,8,128,64]{2,3,1,0:T(8,128)}) %all-gather.12.cloned.1.call-update) | async-done | bytes 1048592 | tf_op jit(solution)/shard_map/all_gather | solution.py:39
  58.3 2.0 multiply_add_fusion.2
  60.5 1.5 broadcast_in_dim.51
  62.0 6.9 %all-to-all-start = ((bf16[8,256,512]{1,2,0:T(8,128)(2,1)}), bf16[8,256,512]{1,2,0:T(8,128)(2,1)S(1)}, u32[]{:S(2)}, u32[]{:S(2)}) async-start(bf16[8,256,512]{1,2,0:T(8,128)(2,1)} %broadcast_in_dim.51), calls=%async_computation | async-start | bytes 4194304 | tf_op jit(solution)/shard_map/all_to_all | solution.py:21
  70.3 7.6 %all-gather.4 = f32[4,1,8]{2,1,0:T(1,128)} all-gather(f32[1,1,8]{2,1,0:T(1,128)S(1)} %get-tuple-element.423), channel_id=1, replica_groups=mesh['seq_0'=4,'seq_1'=4,'seq_2'=2,'head'=8] {'seq_0'}, dimensions={0}, use_global_device_ids=true | all-gather | bytes 160 | tf_op jit(solution)/shard_map/all_gather | solution.py:39
  81.1 6.9 %all-gather.14.cloned.1.call-done = f32[4,8,128,64]{2,3,1,0:T(8,128)} async-done(((f32[1,8,128,64]{2,3,1,0:T(8,128)}), f32[4,8,128,64]{2,3,1,0:T(8,128)}) %all-gather.14.cloned.1.call-update) | async-done | bytes 1048592 | tf_op jit(solution)/shard_map/all_gather | solution.py:39
  88.0 2.7 fusion.103
  90.7 50.4 %while.33 = (s32[]{:T(128)}, f32[8,256,64]{1,2,0:T(8,128)}, f32[8]{0:T(128)}, f32[8,256]{1,0:T(8,128)}, f32[256,256]{1,0:T(8,128)}, /*index=5*/f32[8,256,64]{1,2...) while((s32[]{:T(128)}, f32[8,256,64]{1,2,0:T(8,128)}, f32[8]{0:T(128)}, ...), condition=%wide.region_5.6_spmd.clone, body=%wide.region_2.5_spmd.sunk.clone | while | flops 75956736 | bytes 701625 | solution.py:164
  95.3 1.7 fusion.203
  101.6 1.7 fusion.203
  107.9 1.6 fusion.203
  114.2 1.7 fusion.203
  120.5 1.6 fusion.203
  126.8 1.6 fusion.203
  131.6 1.5 fusion.202
  133.1 1.7 fusion.203
  139.4 1.7 fusion.203
  142.5 1.9 all-gather.16.cloned.1.call-done
  144.4 4.3 multiply_reduce_fusion.5
  148.8 13.1 %all_to_all.29 = f32[8,1,512]{2,1,0:T(1,128)S(1)} all-to-all(f32[8,1,512]{2,1,0:T(1,128)S(1)} %broadcast_in_dim.62), channel_id=1, replica_groups=mesh['seq_0'=4,'seq_1'=4,'seq_2'=2,'head'=8] {'head'}, dimensions={0} | all-to-all | bytes 32768 | tf_op jit(solution)/shard_map/all_to_all | solution.py:21
  162.0 2.3 fusion.85
  165.4 4.1 all-gather.2
  170.4 19.5 %all-gather.18.cloned.1.call-done = f32[4,8,128,64]{2,3,1,0:T(8,128)} async-done(((f32[1,8,128,64]{2,3,1,0:T(8,128)}), f32[4,8,128,64]{2,3,1,0:T(8,128)}) %all-gather.18.cloned.1.call-update) | async-done | bytes 1048592 | tf_op jit(solution)/shard_map/all_gather | solution.py:39
  189.9 2.0 multiply_add_fusion.1
  192.0 7.7 %all-gather.5 = f32[4,1,8]{2,1,0:T(1,128)S(1)} all-gather(f32[1,1,8]{2,1,0:T(1,128)S(1)} %copy-done.20), channel_id=1, replica_groups=mesh['seq_0'=4,'seq_1'=4,'seq_2'=2,'head'=8] {'seq_0'}, dimensions={0}, use_global_device_ids=true | all-gather | bytes 160 | tf_op jit(solution)/shard_map/all_gather | solution.py:39
  201.0 8.6 %all-to-all-start.4 = ((f32[32,1,512]{2,1,0:T(1,128)}), f32[32,1,512]{2,1,0:T(1,128)S(1)}, u32[]{:S(2)}, u32[]{:S(2)}) async-start(f32[32,1,512]{2,1,0:T(1,128)} %broadcast_in_dim.65), calls=%async_computation.4 | async-start | bytes 131072 | tf_op jit(solution)/shard_map/all_to_all | solution.py:21
  209.9 5.8 %convolution_bitcast_fusion.2 = f32[4096,512]{0,1:T(8,128)} fusion(bf16[256,4096]{0,1:T(8,128)(2,1)S(1)} %bitcast.419, f32[256]{0:T(256)S(1)} %get-tuple-element.409, f32[512]{0:T(512)S(1)} %copy-done.9, f32[256,512]{1,0:T(8,128)} %copy-done, bf16[256,512]{1,0:T(8,128)(2,1)} %param.14), kind=kOutput, calls=%fused_computation.104 | convolution fusion | flops 1074921472 | bytes 11275264 | tf_op jit(solution)/shard_map/dot_general | solution.py:204
  215.7 3.6 all-gather.20.cloned.1.call-done
  219.4 1.7 fusion.96
  221.1 152.8 %while.34 = (s32[]{:T(128)}, bf16[8,256,64]{1,2,0:T(8,128)(2,1)S(1)}, f32[8,256,128]{2,1,0:T(8,128)}, f32[8,256,128]{2,1,0:T(8,128)}, f32[8,256]{1,0:T(8,128)}, ...) while((s32[]{:T(128)}, ...), condition=%wide.region_20.21_spmd.clone, body=%wide.region_9.20_spmd.sunk.clone | while | flops 430050560 | bytes 3734389 | solution.py:194
  223.9 1.5 multiply_reduce_fusion.10
  234.5 1.7 fusion.224
  236.2 1.9 multiply_reduce_fusion.11
  243.0 1.5 multiply_reduce_fusion.10
  253.7 1.7 fusion.224
  255.3 1.9 multiply_reduce_fusion.11
  262.2 1.5 multiply_reduce_fusion.10
  272.8 1.7 fusion.224
  274.5 1.9 multiply_reduce_fusion.11
  281.3 1.5 multiply_reduce_fusion.10
  291.9 1.7 fusion.224
  293.6 1.9 multiply_reduce_fusion.11
  300.4 1.5 multiply_reduce_fusion.10
  311.0 1.7 fusion.224
  312.7 1.9 multiply_reduce_fusion.11
  319.5 1.5 multiply_reduce_fusion.10
  330.1 1.7 fusion.224
  331.8 1.9 multiply_reduce_fusion.11
  338.6 1.5 multiply_reduce_fusion.10
  349.2 1.7 fusion.224
  350.9 1.9 multiply_reduce_fusion.11
  357.7 1.5 multiply_reduce_fusion.10
  368.3 1.7 fusion.224
  370.0 1.9 multiply_reduce_fusion.11
  377.1 8.5 %all-to-all-start.3 = ((f32[32,1,8]{2,1,0:T(1,128)}), f32[32,1,8]{2,1,0:T(1,128)S(1)}, u32[]{:S(2)}, u32[]{:S(2)}) async-start(f32[32,1,8]{2,1,0:T(1,128)} %broadcast_in_dim.64), calls=%async_computation.3 | async-start | bytes 32768 | tf_op jit(solution)/shard_map/all_to_all | solution.py:21
  385.6 6.9 %all-to-all-done.3 = f32[32,1,8]{2,1,0:T(1,128)S(1)} async-done(((f32[32,1,8]{2,1,0:T(1,128)}), f32[32,1,8]{2,1,0:T(1,128)S(1)}, u32[]{:S(2)}, u32[]{:S(2)}) %all-to-all-start.3) | async-done | bytes 1056 | tf_op jit(solution)/shard_map/all_to_all | solution.py:21
  392.5 2.5 broadcast_in_dim.63
  395.0 6.7 %all-to-all-start.2 = ((f32[8,1,65536]{2,1,0:T(1,128)}), f32[8,1,65536]{2,1,0:T(1,128)S(1)}, u32[]{:S(2)}, u32[]{:S(2)}) async-start(f32[8,1,65536]{2,1,0:T(1,128)} %broadcast_in_dim.63), calls=%async_computation.2 | async-start | bytes 4194304 | tf_op jit(solution)/shard_map/all_to_all | solution.py:21
  403.7 49.6 %all-to-all-done.2 = f32[8,1,65536]{2,1,0:T(1,128)S(1)} async-done(((f32[8,1,65536]{2,1,0:T(1,128)}), f32[8,1,65536]{2,1,0:T(1,128)S(1)}, u32[]{:S(2)}, u32[]{:S(2)}) %all-to-all-start.2) | async-done | bytes 2097184 | tf_op jit(solution)/shard_map/all_to_all | solution.py:21
  453.3 1.5 reduce_sum.146
  455.6 1.8 copy.63
  (384 shorter events, 161.9 us)
Async XLA Ops:
  7.2 10.4 %copy-start.23 = (u32[256]{0:T(256)S(1)}, u32[256]{0:T(256)}, u32[]{:S(2)}) copy-start(u32[256]{0:T(256)} %constant.104) | copy-start | bytes 3076
  7.2 11.0 %copy-start.22 = (u32[256]{0:T(256)S(1)}, u32[256]{0:T(256)}, u32[]{:S(2)}) copy-start(u32[256]{0:T(256)} %constant.99) | copy-start | bytes 3076
  7.2 51.1 %all-gather.12.cloned.1.call-start = ((), (), s32[]{:S(2)}) async-start(), calls=%async_computation.6 | async-start | bytes 1310720 | tf_op jit(solution)/shard_map/all_gather | solution.py:39
  8.3 3.5 copy-start.4
  11.8 48.5 %copy-start.6 = (bf16[256,512]{1,0:T(8,128)(2,1)S(1)}, bf16[256,512]{1,0:T(8,128)(2,1)}, u32[]{:S(2)}) copy-start(bf16[256,512]{1,0:T(8,128)(2,1)} %param.21) | copy-start | bytes 786436
  30.3 0.9 copy-start.16
  30.3 0.9 copy-start.17
  30.3 31.7 %copy-start.13 = (f32[8]{0:T(128)}, f32[8]{0:T(128)S(1)}, u32[]{:S(2)}) copy-start(f32[8]{0:T(128)S(1)} %get-tuple-element.420) | copy-start | bytes 100
  31.1 56.9 %all-gather.14.cloned.1.call-start = ((), (), s32[]{:S(2)}) async-start(), calls=%async_computation.7 | async-start | bytes 1310720 | tf_op jit(solution)/shard_map/all_gather | solution.py:39
  31.9 30.1 %copy-start.11 = (f32[8]{0:T(128)}, f32[8]{0:T(128)S(1)}, u32[]{:S(2)}) copy-start(f32[8]{0:T(128)S(1)} %get-tuple-element.426) | copy-start | bytes 100
  62.0 17.0 %copy-start.7 = (bf16[256,128]{1,0:T(8,128)(2,1)S(1)}, bf16[256,128]{1,0:T(8,128)(2,1)}, u32[]{:S(2)}) copy-start(bf16[256,128]{1,0:T(8,128)(2,1)} %param.16) | copy-start | bytes 196612
  62.0 18.3 %copy-start.8 = (bf16[256,128]{1,0:T(8,128)(2,1)S(1)}, bf16[256,128]{1,0:T(8,128)(2,1)}, u32[]{:S(2)}) copy-start(bf16[256,128]{1,0:T(8,128)(2,1)} %param.15) | copy-start | bytes 196612
  62.0 80.5 %all-to-all-start = ((bf16[8,256,512]{1,2,0:T(8,128)(2,1)}), bf16[8,256,512]{1,2,0:T(8,128)(2,1)S(1)}, u32[]{:S(2)}, u32[]{:S(2)}) async-start(bf16[8,256,512]{1,2,0:T(8,128)(2,1)} %broadcast_in_dim.51), calls=%async_computation | async-start | bytes 4194304 | tf_op jit(solution)/shard_map/all_to_all | solution.py:21
  68.9 75.6 %all-gather.16.cloned.1.call-start = ((), (), s32[]{:S(2)}) async-start(), calls=%async_computation.8 | async-start | bytes 4325376 | tf_op jit(solution)/shard_map/all_gather | solution.py:151
  69.6 120.3 %all-gather.18.cloned.1.call-start = ((), (), s32[]{:S(2)}) async-start(), calls=%async_computation.9 | async-start | bytes 1310720 | tf_op jit(solution)/shard_map/all_gather | solution.py:39
  90.7 53.7 %copy-start.9 = (f32[512]{0:T(512)S(1)}, f32[512]{0:T(512)}, u32[]{:S(2)}) copy-start(f32[512]{0:T(512)} %param.19) | copy-start | bytes 6148
  141.1 7.7 %copy-start.1 = (f32[8,256,64]{1,2,0:T(8,128)}, f32[8,256,64]{1,2,0:T(8,128)S(1)}, u32[]{:S(2)}) copy-start(f32[8,256,64]{1,2,0:T(8,128)S(1)} %get-tuple-element.754) | copy-start | bytes 1572868
  142.5 19.4 %copy-start = (f32[256,512]{1,0:T(8,128)}, f32[256,512]{1,0:T(8,128)S(1)}, u32[]{:S(2)}) copy-start(f32[256,512]{1,0:T(8,128)S(1)} %copy.54) | copy-start | bytes 1572868
  161.9 7.6 %copy-start.14 = (f32[8]{0:T(128)S(1)}, f32[8]{0:T(128)}, u32[]{:S(2)}) copy-start(f32[8]{0:T(128)} %get-tuple-element.415) | copy-start | bytes 100
  161.9 7.5 %copy-start.15 = (f32[8]{0:T(128)S(1)}, f32[8]{0:T(128)}, u32[]{:S(2)}) copy-start(f32[8]{0:T(128)} %get-tuple-element.418) | copy-start | bytes 100
  164.2 25.7 %copy-start.10 = (f32[8]{0:T(128)S(1)}, f32[8]{0:T(128)}, u32[]{:S(2)}) copy-start(f32[8]{0:T(128)} %get-tuple-element.424) | copy-start | bytes 100
  164.2 25.7 %copy-start.12 = (f32[8]{0:T(128)S(1)}, f32[8]{0:T(128)}, u32[]{:S(2)}) copy-start(f32[8]{0:T(128)} %get-tuple-element.419) | copy-start | bytes 100
  164.4 27.5 %copy-start.20 = (f32[1,1,8]{2,1,0:T(1,128)S(1)}, f32[1,1,8]{2,1,0:T(1,128)}, u32[]{:S(2)}) copy-start(f32[1,1,8]{2,1,0:T(1,128)} %get-tuple-element.422) | copy-start | bytes 100
  170.3 49.0 %all-gather.20.cloned.1.call-start = ((), (), s32[]{:S(2)}) async-start(), calls=%async_computation.10 | async-start | bytes 1310720 | tf_op jit(solution)/shard_map/all_gather | solution.py:39
  201.0 175.5 %all-to-all-start.4 = ((f32[32,1,512]{2,1,0:T(1,128)}), f32[32,1,512]{2,1,0:T(1,128)S(1)}, u32[]{:S(2)}, u32[]{:S(2)}) async-start(f32[32,1,512]{2,1,0:T(1,128)} %broadcast_in_dim.65), calls=%async_computation.4 | async-start | bytes 131072 | tf_op jit(solution)/shard_map/all_to_all | solution.py:21
  209.6 246.0 %reduce-scatter.2.cloned.1.call-start = ((), (), s32[]{:S(2)}) async-start(), calls=%async_computation.11 | async-start | bytes 8650752 | tf_op jit(solution)/shard_map/reduce_scatter | solution.py:203
  215.7 3.7 copy-start.3
  215.7 3.7 copy-start.18
  215.7 3.7 copy-start.19
  215.7 5.4 %copy-start.2 = (f32[8,256,64]{1,2,0:T(8,128)S(1)}, f32[8,256,64]{1,2,0:T(8,128)}, u32[]{:S(2)}) copy-start(f32[8,256,64]{1,2,0:T(8,128)} %copy-done.1) | copy-start | bytes 1572868
  215.7 5.4 %copy-start.5 = (bf16[8,256,64]{1,2,0:T(8,128)(2,1)S(1)}, bf16[8,256,64]{1,2,0:T(8,128)(2,1)}, u32[]{:S(2)}) copy-start(bf16[8,256,64]{1,2,0:T(8,128)(2,1)} %broadcast_convert_fusion) | copy-start | bytes 786436
  215.7 5.4 %copy-start.21 = (f32[8]{0:T(128)S(1)}, f32[8]{0:T(128)}, u32[]{:S(2)}) copy-start(f32[8]{0:T(128)} %get-tuple-element.775) | copy-start | bytes 100
  377.1 15.4 %all-to-all-start.3 = ((f32[32,1,8]{2,1,0:T(1,128)}), f32[32,1,8]{2,1,0:T(1,128)S(1)}, u32[]{:S(2)}, u32[]{:S(2)}) async-start(f32[32,1,8]{2,1,0:T(1,128)} %broadcast_in_dim.64), calls=%async_computation.3 | async-start | bytes 32768 | tf_op jit(solution)/shard_map/all_to_all | solution.py:21
  395.0 58.4 %all-to-all-start.2 = ((f32[8,1,65536]{2,1,0:T(1,128)}), f32[8,1,65536]{2,1,0:T(1,128)S(1)}, u32[]{:S(2)}, u32[]{:S(2)}) async-start(f32[8,1,65536]{2,1,0:T(1,128)} %broadcast_in_dim.63), calls=%async_computation.2 | async-start | bytes 4194304 | tf_op jit(solution)/shard_map/all_to_all | solution.py:21
Sparse Core Ops, SparseCore 0:
  31.2 27.0 all-gather.11
  60.7 27.2 all-gather.13
  90.5 53.8 all-gather.15
  170.4 19.4 all-gather.17
  192.1 27.2 all-gather.19
  223.2 100.9 reduce-scatter.1
where the time goes:
time: 470 us; the launch traced here: 464 us
  matrix products  116 us (25%)
  waiting for transfers between devices  116 us (25%)
  other arithmetic  78.1 us (17%)
  local copies, waits for them, and re-layouts  50.1 us (11%)
  blocking collectives  46.8 us (10%)
  starting transfers between devices  31 us (7%)
  between operations  15.8 us (3%)
  loops' own time  11.2 us (2%)
    dot_general x65, matrix products, dot_high(): jnp.dot(left, right, precision=lax.Precision.HIGHEST, preferred_element_t...  69.1 us
    all_to_all x4, waiting for transfers between devices, copy_for_each(): lax.all_to_all(jnp.broadcast_to(x[None], (peers, *x.shape)), axis, 0, 0,...  56.5 us
    all_gather x4, waiting for transfers between devices, entering(): pieces = jax.tree.map(lambda part: lax.all_gather(part, axis), so_far)  56.5 us
    dot_general x26, matrix products, dot_inner(): lax.dot_general(left, right, (((0,), (0,)), ((), ())), precision=lax.Prec...  36.5 us
    all_to_all x4, starting transfers between devices, copy_for_each(): lax.all_to_all(jnp.broadcast_to(x[None], (peers, *x.shape)), axis, 0, 0,...  30.6 us
    all_gather x4, blocking collectives, entering(): pieces = jax.tree.map(lambda part: lax.all_gather(part, axis), so_far)  24.4 us
    mul x16, other arithmetic, decay_table(): logs = -jnp.cumsum(rate * step)  21.6 us
    reduce_sum x8, other arithmetic, span_backward(): rate_part = -jnp.sum(step * log_grad)  15.1 us
  transfers between devices with their start and end apart: 10, of which 7 were waited for; matrix products, arithmetic and copies ran while one was open for 48% of the time, Pallas kernels for 0%

commit v1 on v0

v1 whole, which is shorter than its diff:
```python
import jax
import jax.numpy as jnp
from jax import lax
from jax.experimental import pallas as pl
from jax.experimental.pallas import tpu as pltpu
from jax.sharding import Mesh
from jax.sharding import PartitionSpec as P

SEQ = ("seq_0", "seq_1", "seq_2")
EPSILON = 1e-05
MESH = pl.DeviceIdType.MESH
BF = jnp.bfloat16
F32 = jnp.float32


def mm(a, b):
    return jnp.dot(a, b, preferred_element_type=F32)


def nt(a, b):
    return lax.dot_general(a, b, (((1,), (1,)), ((), ())), preferred_element_type=F32)


def split2(v):
    hi = v.astype(BF)
    return hi, (v - hi.astype(F32)).astype(BF)


def split3(v):
    hi = v.astype(BF)
    rest = v - hi.astype(F32)
    mid = rest.astype(BF)
    return hi, mid, (rest - mid.astype(F32)).astype(BF)


def lanes(*parts):
    return jnp.concatenate(parts, axis=1)


def rows(*parts):
    return jnp.concatenate(parts, axis=0)


def kernel(
    x_ref, z_ref, b_ref, c_ref, step_ref, rate_ref, gain_ref, w_ref, g_ref,
    gx_ref, gz_ref, gb_ref, gc_ref, gs_ref, gr_ref, gg_ref, gw_ref,
    gfull, wbuf, dec_src, dec_all, st_send, st_recv, st_pref, st_in,
    ad_send, ad_recv, ad_pref, ad_in, stat_src, stat_all,
    pt_own, pt_send, pt_recv, rs_o, rs_p, rs_m, buf_p, buf_m, fin,
    tot, t_o, t_p, t_m, tbuf_p, tbuf_m, tfin,
    cpart, crecv, csum, call_, bpart, brecv, bsum, ball,
    gg_src, gg_all, rt_src, rt_all,
    rate_c, lg, lgt, stept, fr, stl, xs2, sc, sct, mix_t, mix_b, ybuf, ycs, gn,
    nb, ntr, ehi, elo, ef2, rprod, colst, ws, qcol, rowp, gxi, mixw, pprod,
    zs, zr, w1s, w1r, w2s, w2r, wds, wdr, des, der, a1s, a1r, a2s, a2r,
    b1s, b1r, b2s, b2r, sts, str_, d0s, d0r, r1s, r1r, r2s, r2r,
    c1s, c1r, c2s, c2r, k1s, k1r, k2s, k2r, ggs, ggr, rts, rtr,
):
    y = lax.axis_index("seq_0")
    x = lax.axis_index("seq_1")
    c = lax.axis_index("seq_2")
    z = lax.axis_index("head")
    me = (y * 4 + x) * 2 + c
    oc = 1 - c
    q = x * oc + y * c
    p = y * oc + x * c
    group = y * 4 + x

    def at_seq(k):
        return (k // 8, (k // 2) % 4, k % 2, z)

    def at_head(k):
        return (y, x, c, k)

    def first(d):
        return ((y + d * c) % 4, (x + d * oc) % 4, c, z)

    def second(d):
        return ((y + d * oc) % 4, (x + d * c) % 4, c, z)

    partner = (y, x, oc, z)

    def copy(src, dst, ssem, rsem, dev):
        return pltpu.make_async_remote_copy(
            src_ref=src, dst_ref=dst, send_sem=ssem, recv_sem=rsem,
            device_id=dev, device_id_type=MESH,
        )

    def got(ref, sem):
        copy(ref, ref, sem, sem, partner).wait_recv()

    sent = []

    def send(src, dst, ssem, rsem, dev):
        d = copy(src, dst, ssem, rsem, dev)
        d.start()
        sent.append(d)

    def to_seq(make):
        def one(d, carry):
            k = (me + d) % 32
            make(k).start()
            return carry

        lax.fori_loop(1, 32, one, 0)

    def to_head(make):
        for d in range(1, 8):
            make((z + d) % 8).start()

    barrier = pltpu.get_barrier_semaphore()

    def greet(d, carry):
        pl.semaphore_signal(barrier, inc=1, device_id=at_seq((me + d) % 32), device_id_type=MESH)
        return carry

    lax.fori_loop(1, 32, greet, 0)
    for d in range(1, 8):
        pl.semaphore_signal(barrier, inc=1, device_id=at_head((z + d) % 8), device_id_type=MESH)

    i8 = lax.broadcasted_iota(jnp.int32, (8, 8), 0)
    j8 = lax.broadcasted_iota(jnp.int32, (8, 8), 1)
    rate = jnp.sum(jnp.where(i8 == j8, jnp.broadcast_to(rate_ref[...], (8, 8)), 0.0), axis=1, keepdims=True)
    rate_c[...] = jnp.broadcast_to(rate, (8, 128))
    step = step_ref[...]
    ia = lax.broadcasted_iota(jnp.int32, (256, 256), 0)
    ib = lax.broadcasted_iota(jnp.int32, (256, 256), 1)
    tri_u = jnp.where(ia <= ib, 1.0, 0.0).astype(BF)
    v1, v2, v3 = split3(rate * step)
    logs = -(mm(v1, tri_u) + mm(v2, tri_u) + mm(v3, tri_u))
    lg[...] = logs
    logs_t = jnp.transpose(logs)
    step_t = jnp.transpose(step)
    lgt[:, 0:8] = logs_t
    stept[:, 0:8] = step_t
    e8 = jnp.where(
        lax.broadcasted_iota(jnp.int32, (8, 512), 0)
        == lax.broadcasted_iota(jnp.int32, (8, 512), 1) // 64, 1.0, 0.0,
    ).astype(BF)

    def spread_heads(v):
        a1, a2, a3 = split3(v)
        return mm(a1, e8) + mm(a2, e8) + mm(a3, e8)

    fr[...] = spread_heads(jnp.exp(logs_t))
    stl[...] = spread_heads(step_t * jnp.exp(logs_t[255:256, :] - logs_t))
    dec_src[0] = fr[255:256, :]
    dec_all[me] = fr[255:256, :]
    bt = b_ref[...].T
    ct = c_ref[...].T
    for r in range(4):
        rs = slice(64 * r, 64 * r + 64)
        hi, lo = split2(x_ref[rs, :].astype(F32) * stl[rs, :])
        xs2[rs, :] = hi
        xs2[64 * r + 256 : 64 * r + 320, :] = lo
    st_send[...] = mm(lanes(bt, bt), xs2[...])

    pl.semaphore_wait(barrier, 38)

    for k in range(2):
        rk = pl.ds(128 * k, 128)
        for side, d in ((0, 1), (1, 7)):
            send(g_ref.at[rk], gfull.at[z, rk], zs.at[side, 0, k], zr.at[side, 0, k], at_head((z + d) % 8))
    for side, d in ((0, 1), (1, 3)):
        send(w_ref, wbuf.at[c, p, q], w1s.at[side], w1r.at[side], first(d))
    to_seq(lambda k: copy(dec_src.at[0], dec_all.at[me], des, der, at_seq(k)))

    def slab(ref, k):
        return ref.at[
            pl.ds(pl.multiple_of(8 * (k // 2), 8), 8),
            pl.ds(pl.multiple_of(256 * (k % 2), 256), 256),
        ]

    to_seq(lambda k: copy(slab(st_send, k), st_recv.at[me], a1s, a1r, at_seq(k)))
    st_recv[me] = slab(st_send, me)[...]
    gfull[z] = g_ref[...]
    wbuf[c, p, q] = w_ref[...]

    iota_i = lax.broadcasted_iota(jnp.int32, (64, 256), 0)
    iota_j = lax.broadcasted_iota(jnp.int32, (64, 256), 1)
    raw = mm(c_ref[...], bt)
    for r in range(4):
        rs = slice(64 * r, 64 * r + 64)
        sc[rs, :] = jnp.where(iota_i + 64 * r >= iota_j, raw[rs, :], 0.0)
    sct[...] = mm(b_ref[...], ct)

    qm, qp, q2 = (q + 3) % 4, (q + 1) % 4, (q + 2) % 4
    pm, pp, p2 = (p + 3) % 4, (p + 1) % 4, (p + 2) % 4
    got(wbuf.at[c, p, qm], w1r.at[0])
    top = pl.ds(0, 64)
    send(wbuf.at[c, p, qm, top], wbuf.at[c, p, qm, top], w1s.at[2], w1r.at[2], first(1))
    got(wbuf.at[c, p, qp], w1r.at[1])
    low = pl.ds(64, 64)
    send(wbuf.at[c, p, qp, low], wbuf.at[c, p, qp, low], w1s.at[3], w1r.at[3], first(3))

    half = lax.broadcasted_iota(jnp.int32, (1, 128), 1)
    keep = (
        jnp.where(half < 64, 1.0, 0.0).astype(BF),
        jnp.where(half < 64, 0.0, 1.0).astype(BF),
    )

    def inside(hp):
        ls = slice(128 * hp, 128 * hp + 128)
        mt, mb = mix_t.at[hp % 2], mix_b.at[hp % 2]
        xp = x_ref[:, ls]
        x0, x1 = xp * keep[0], xp * keep[1]
        for k in range(2):
            h = 2 * hp + k
            for r in range(4):
                rs = slice(64 * r, 64 * r + 64)
                wd = 128 if r < 2 else 256
                t = jnp.exp(jnp.minimum(lgt[rs, h : h + 1] - lg[h : h + 1, 0:wd], 0.0))
                hi, lo = split2(t * (sc[rs, 0:wd] * step_ref[h : h + 1, 0:wd]))
                dst = mt if r < 2 else mb
                rr = slice(64 * (r % 2), 64 * (r % 2) + 64)
                dst[rr, 2 * k * wd : (2 * k + 1) * wd] = hi
                dst[rr, (2 * k + 1) * wd : (2 * k + 2) * wd] = lo
        ybuf[0:128, ls] = mm(mt[...], rows(x0[0:128], x0[0:128], x1[0:128], x1[0:128]))
        ybuf[128:256, ls] = mm(mb[...], rows(x0, x0, x1, x1))

    def z_block(side, j):
        return (z + 8 - j) % 8 if side == 0 else (z + j) % 8

    def z_forward(j):
        for k in range(2):
            rk = pl.ds(128 * k, 128)
            for side, d in ((0, 1), (1, 7)):
                blk = gfull.at[z_block(side, j), rk]
                got(blk, zr.at[side, j - 1, k])
                if j < 3 or k == side:
                    send(blk, blk, zs.at[side, j, k], zr.at[side, j, k], at_head((z + d) % 8))

    def scan(recv, pref, back):
        s = jnp.zeros((8, 256), F32)
        for k in reversed(range(32)) if back else range(32):
            pref[k] = s
            s = s * dec_all[k, :, pl.ds(pl.multiple_of(256 * c, 256), 256)] + recv[k]

    many = pl.ds(0, 31)

    inside(0)
    inside(1)
    got(dec_all.at[many], der)
    got(st_recv.at[many], a1r)
    scan(st_recv, st_pref, False)
    to_seq(lambda k: copy(st_pref.at[k], slab(st_in, me), a2s, a2r, at_seq(k)))
    slab(st_in, me)[...] = st_pref[me]

    got(wbuf.at[c, p, q2, top], w1r.at[2])
    got(wbuf.at[c, p, q2, low], w1r.at[3])
    mine = wbuf.at[c, p]
    for side, d in ((0, 1), (1, 3)):
        send(mine, mine, w2s.at[side], w2r.at[side], second(d))
    send(mine, mine, wds.at[0], wdr.at[0], partner)
    inside(2)
    z_forward(1)
    inside(3)

    got(st_recv.at[many], a2r)
    s_hi, s_lo = split2(st_in[...])
    cc = lanes(c_ref[...], c_ref[...])
    for r in range(4):
        rs = slice(64 * r, 64 * r + 64)
        v = fr[rs, :] * mm(cc[rs, :], rows(s_hi, s_lo))
        ycs[rs, :] = v
        ybuf[rs, :] = ybuf[rs, :] + v
    z_forward(2)

    ab, cd = pl.ds(0, 2), pl.ds(2, 2)
    got(wbuf.at[c, pm], w2r.at[0])
    send(wbuf.at[c, pm, ab], wbuf.at[c, pm, ab], w2s.at[2], w2r.at[2], second(1))
    send(wbuf.at[c, pm], wbuf.at[c, pm], wds.at[1], wdr.at[1], partner)
    got(wbuf.at[c, pp], w2r.at[1])
    send(wbuf.at[c, pp, cd], wbuf.at[c, pp, cd], w2s.at[3], w2r.at[3], second(3))
    send(wbuf.at[c, pp], wbuf.at[c, pp], wds.at[2], wdr.at[2], partner)
    z_forward(3)
    got(wbuf.at[c, p2, ab], w2r.at[2])
    send(wbuf.at[c, p2, ab], wbuf.at[c, p2, ab], wds.at[3], wdr.at[3], partner)
    got(wbuf.at[c, p2, cd], w2r.at[3])
    send(wbuf.at[c, p2, cd], wbuf.at[c, p2, cd], wds.at[4], wdr.at[4], partner)
    for side in range(2):
        got(gfull.at[z_block(side, 4), pl.ds(128 * side, 128)], zr.at[side, 3, side])
    for n in range(3):
        got(wbuf.at[oc, p], wdr.at[n])
    got(wbuf.at[oc, p, ab], wdr.at[3])
    got(wbuf.at[oc, p, cd], wdr.at[4])

    for r in range(2):
        rs = slice(128 * r, 128 * r + 128)
        acc = None
        for cp in range(2):
            for i2 in range(4):
                parts = []
                for i1 in range(4):
                    yy, xx = (i2, i1) if cp == 0 else (i1, i2)
                    off = (xx % 2) * 256 + cp * 128
                    parts.append(gfull[2 * yy + xx // 2, rs, off : off + 128])
                part = mm(lanes(*parts), wbuf[cp, i2].reshape(512, 512))
                acc = part if acc is None else acc + part
        gn[rs, :] = acc

    gain = gain_ref[...]

    def folded(v):
        return v[:, 0:128] + v[:, 128:256] + v[:, 256:384] + v[:, 384:512]

    for r in range(4):
        rs = slice(64 * r, 64 * r + 64)
        zf = z_ref[rs, :].astype(F32)
        u = ybuf[rs, :] * (zf / (1.0 + jnp.exp(-zf)))
        pprod[rs, 0:128] = folded(u * u)
        pprod[rs, 128:256] = folded(gn[rs, :] * gain * u)
    stat_src[0:1, :] = jnp.sum(jnp.transpose(pprod[:, 0:128]), axis=0, keepdims=True)
    stat_src[1:2, :] = jnp.sum(jnp.transpose(pprod[:, 128:256]), axis=0, keepdims=True)
    stat_all[z] = stat_src[...]
    to_head(lambda k: copy(stat_src, stat_all.at[z], sts, str_, at_head(k)))
    got(stat_all.at[pl.ds(0, 7)], str_)
    stats = jnp.sum(stat_all[...], axis=0)
    inv_row = lax.rsqrt(stats[0:1, :] / 4096.0 + EPSILON)
    coef_row = inv_row * inv_row * (stats[1:2, :] / 4096.0)
    colst[:, 0:8] = jnp.transpose(rows(inv_row, coef_row, jnp.zeros((6, 256), F32)))

    gg_acc = jnp.zeros((8, 512), F32)
    for r in range(8):
        rs = slice(32 * r, 32 * r + 32)
        inv, coef = colst[rs, 0:1], colst[rs, 1:2]
        zf = z_ref[rs, :].astype(F32)
        s = 1.0 / (1.0 + jnp.exp(-zf))
        sil = zf * s
        yv = ybuf[rs, :]
        gnv = gn[rs, :]
        ui = yv * sil * inv
        nb[rs, :] = (ui * gain).astype(BF)
        gg_acc = gg_acc + jnp.sum((gnv * ui).reshape(4, 8, 512), axis=0)
        gu = inv * (gnv * gain - yv * sil * coef)
        e = gu * sil
        gz_ref[rs, :] = (gu * yv * s * (1.0 + zf * (1.0 - s))).astype(BF)
        hi, lo = split2(e)
        ehi[rs, :] = hi
        elo[rs, :] = lo
        hi, lo = split2(e * fr[rs, :])
        ef2[rs, :] = hi
        ef2[256 + 32 * r : 288 + 32 * r, :] = lo
        hi, lo = split2(e * ycs[rs, :])
        rprod[rs, 0:512] = hi
        rprod[rs, 512:1024] = lo
    ad_send[...] = mm(lanes(ct, ct), ef2[...])
    to_seq(lambda k: copy(slab(ad_send, k), ad_recv.at[me], b1s, b1r, at_seq(k)))
    ad_recv[me] = slab(ad_send, me)[...]
    gg_src[0] = jnp.sum(gg_acc, axis=0, keepdims=True)
    gg_all[me] = gg_src[0]
    to_seq(lambda k: copy(gg_src.at[0], gg_all.at[me], ggs, ggr, at_seq(k)))

    ntr[...] = nb[...].T

    def one_chip(i, carry):
        yy, xx = i // 4, i % 4
        blk = 2 * yy + xx // 2
        base = (xx % 2) * 256
        left = gfull[blk, :, pl.ds(pl.multiple_of(base + 128 * c, 128), 128)]
        right = gfull[blk, :, pl.ds(pl.multiple_of(base + 128 * oc, 128), 128)]
        both = mm(ntr[...], lanes(left, right))
        own1, own2 = xx * oc + yy * c, yy * oc + xx * c
        pt_own[own2, own1] = both[:, 0:128]
        pt_send[own1, own2] = both[:, 128:256].astype(BF)
        return carry

    lax.fori_loop(0, 16, one_chip, 0)
    order = (2, 1, 3, 0)
    for n in range(4):
        i2 = (q + order[n]) % 4
        send(pt_send.at[i2], pt_recv.at[i2], d0s.at[n], d0r.at[n], partner)

    mask_t = (iota_j >= iota_i, iota_j >= iota_i + 64)
    mask_b = (iota_j[:, 0:128] >= iota_i[:, 0:128], iota_j[:, 0:128] >= iota_i[:, 0:128] + 64)

    def inside_back(hp):
        ls = slice(128 * hp, 128 * hp + 128)
        mw = mixw.at[hp % 2]
        xp = x_ref[:, ls]
        eh, el = ehi[:, ls], elo[:, ls]
        e2 = lanes(eh, el)
        for k in range(2):
            h = 2 * hp + k
            xk = xp * keep[k]
            x2 = lanes(xk, xk)
            inner_t = nt(x2[0:128], e2)
            inner_b = nt(x2[128:256], e2[128:256])
            racc_l = jnp.zeros((1, 128), F32)
            racc_r = jnp.zeros((1, 128), F32)
            for r in range(4):
                rs = slice(64 * r, 64 * r + 64)
                rr = slice(64 * (r % 2), 64 * (r % 2) + 64)
                cs = slice(0, 256) if r < 2 else slice(128, 256)
                t = jnp.exp(jnp.minimum(lg[h : h + 1, cs] - lgt[rs, h : h + 1], 0.0))
                tab = jnp.where(mask_t[r] if r < 2 else mask_b[r - 2], t, 0.0)
                inner = inner_t[rr] if r < 2 else inner_b[rr]
                st = sct[rs, cs]
                sj = stept[rs, h : h + 1]
                w = tab * inner
                sw = w * sj
                if r < 2:
                    mw[rr, 256 * k : 256 * k + 256] = (tab * st * sj).astype(BF)
                else:
                    mw[128 + 64 * (r - 2) : 192 + 64 * (r - 2), 128 * k : 128 * k + 128] = (tab * st * sj).astype(BF)
                qcol[rs, h : h + 1] = jnp.sum(w * st, axis=1, keepdims=True)
                if h == 0:
                    ws[rs, cs] = sw
                else:
                    ws[rs, cs] = ws[rs, cs] + sw
                rsum = jnp.sum(sw * st, axis=0, keepdims=True)
                if r < 2:
                    racc_l = racc_l + rsum[:, 0:128]
                    racc_r = racc_r + rsum[:, 128:256]
                else:
                    racc_r = racc_r + rsum
            rowp[h : h + 1, 0:128] = racc_l
            rowp[h : h + 1, 128:256] = racc_r
        em0, em1 = lanes(eh * keep[0], el * keep[0]), lanes(eh * keep[1], el * keep[1])
        v = mm(mw[0:128, :], rows(em0, em1))
        gxi[0:128, ls] = v[:, 0:128] + v[:, 128:256]
        v = mm(mw[128:256, 0:256], rows(em0[128:256], em1[128:256]))
        gxi[128:256, ls] = v[:, 0:128] + v[:, 128:256]

    inside_back(0)
    got(pt_recv.at[p2], d0r.at[0])
    for i in range(4):
        rs_o[i] = (pt_own[p2, i] + pt_recv[p2, i].astype(F32)).astype(BF)
    send(rs_o.at[ab], buf_p, r1s.at[0], r1r.at[0], second(1))
    send(rs_o.at[cd], buf_m, r1s.at[1], r1r.at[1], second(3))
    inside_back(1)
    inside_back(2)
    inside_back(3)

    got(ad_recv.at[many], b1r)
    scan(ad_recv, ad_pref, True)
    to_seq(lambda k: copy(ad_pref.at[k], slab(ad_in, me), b2s, b2r, at_seq(k)))
    slab(ad_in, me)[...] = ad_pref[me]

    got(pt_recv.at[pp], d0r.at[1])
    for i in range(4):
        v = pt_own[pp, i] + pt_recv[pp, i].astype(F32)
        if i < 2:
            pt_own[pp, i] = v
        else:
            rs_p[i] = v.astype(BF)
    send(rs_p.at[cd], fin.at[0, cd], r1s.at[2], r1r.at[2], second(1))
    got(pt_recv.at[pm], d0r.at[2])
    for i in range(4):
        v = pt_own[pm, i] + pt_recv[pm, i].astype(F32)
        if i < 2:
            rs_m[i] = v.astype(BF)
        else:
            pt_own[pm, i] = v
    send(rs_m.at[ab], fin.at[1, ab], r1s.at[3], r1r.at[3], second(3))

    ws[128:256, 0:128] = jnp.zeros((128, 128), F32)
    w_hi, w_lo = split2(jnp.transpose(ws[...]))
    gq = mm(lanes(w_hi, w_lo), rows(b_ref[...], b_ref[...]))
    gq = gq + nt(lanes(ef2[0:256], ef2[256:512], ef2[0:256]), lanes(s_hi, s_hi, s_lo))
    for k in range(8):
        cpart[k] = gq[32 * k : 32 * k + 32]
    crecv[z] = cpart[z]
    to_head(lambda k: copy(cpart.at[k], crecv.at[z], c1s, c1r, at_head(k)))
    w_hi, w_lo = split2(ws[...])
    gk = mm(lanes(w_hi, w_lo), rows(c_ref[...], c_ref[...]))

    got(pt_recv.at[p], d0r.at[3])
    for i in range(4):
        pt_own[p, i] = pt_own[p, i] + pt_recv[p, i].astype(F32)

    got(buf_p, r1r.at[0])
    for i in range(2):
        rs_p[i] = (pt_own[pp, i] + buf_p[i].astype(F32)).astype(BF)
    send(rs_p.at[ab], fin.at[0, ab], r2s.at[0], r2r.at[0], second(1))
    got(buf_m, r1r.at[1])
    for i in range(2):
        rs_m[2 + i] = (pt_own[pm, 2 + i] + buf_m[i].astype(F32)).astype(BF)
    send(rs_m.at[cd], fin.at[1, cd], r2s.at[1], r2r.at[1], second(3))

    got(ad_recv.at[many], b2r)
    a_hi, a_lo = split2(ad_in[...])
    gk = gk + nt(lanes(xs2[0:256], xs2[256:512], xs2[0:256]), lanes(a_hi, a_hi, a_lo))
    for k in range(8):
        bpart[k] = gk[32 * k : 32 * k + 32]
    brecv[z] = bpart[z]
    to_head(lambda k: copy(bpart.at[k], brecv.at[z], k1s, k1r, at_head(k)))
    got(crecv.at[pl.ds(0, 7)], c1r)
    csum[...] = jnp.sum(crecv[...], axis=0)
    call_[z] = csum[...]
    to_head(lambda k: copy(csum, call_.at[z], c2s, c2r, at_head(k)))

    bb = lanes(b_ref[...], b_ref[...])
    for r in range(4):
        rs = slice(64 * r, 64 * r + 64)
        ka = mm(bb[rs, :], rows(a_hi, a_lo))
        gx_ref[rs, :] = (gxi[rs, :] + stl[rs, :] * ka).astype(BF)
        hi, lo = split2(x_ref[rs, :].astype(F32) * ka)
        pprod[rs, 0:512] = hi.astype(F32)
        pprod[rs, 512:1024] = lo.astype(F32)
    e16 = lanes(e8, e8)
    carr = nt(e16, pprod[...].astype(BF))
    rstate = nt(e16, rprod[...])
    held = jnp.sum((ad_in[...] * st_in[...]).reshape(16, 8, 512), axis=0)
    h_hi, h_lo = split2(held)
    held8 = jnp.sum(nt(e16, lanes(h_hi, h_lo)), axis=1, keepdims=True)
    logs = lg[...]
    step = step_ref[...]
    rate = rate_c[:, 0:1]
    tail = jnp.exp(logs[:, 255:256] - logs)
    q_in = jnp.transpose(qcol[...])[0:8, :]
    tc = tail * carr
    q_terms = q_in + tc
    drive = rowp[...] + rstate - step * q_terms
    boundary = jnp.exp(logs[:, 255:256]) * held8 + jnp.sum(step * tc, axis=1, keepdims=True)
    tri_l = jnp.where(ia >= ib, 1.0, 0.0).astype(BF)
    v1, v2, v3 = split3(drive)
    log_grad = mm(v1, tri_l) + mm(v2, tri_l) + mm(v3, tri_l) + boundary
    gs_ref[...] = q_terms - rate * log_grad
    rp = -jnp.sum(step * log_grad, axis=1, keepdims=True)
    d0 = lax.broadcasted_iota(jnp.int32, (8, 128), 0)
    d1 = lax.broadcasted_iota(jnp.int32, (8, 128), 1)
    rt_src[0] = jnp.sum(jnp.where(d0 == d1, rp, 0.0), axis=0, keepdims=True)
    rt_all[me] = rt_src[0]
    to_seq(lambda k: copy(rt_src.at[0], rt_all.at[me], rts, rtr, at_seq(k)))

    got(fin.at[0, cd], r1r.at[2])
    got(fin.at[1, ab], r1r.at[3])
    got(fin.at[0, ab], r2r.at[0])
    got(fin.at[1, cd], r2r.at[1])

    def total(i):
        return pt_own[p, i] + fin[0, i].astype(F32) + fin[1, i].astype(F32)

    hi_rows, lo_rows = pl.ds(0, 256), pl.ds(256, 256)
    t_o[...] = total(q2).astype(BF)
    send(t_o.at[hi_rows], tbuf_p, r1s.at[4], r1r.at[4], first(1))
    send(t_o.at[lo_rows], tbuf_m, r1s.at[5], r1r.at[5], first(3))
    v = total(qp)
    tot[0] = v[0:256]
    t_p[256:512, :] = v[256:512].astype(BF)
    send(t_p.at[lo_rows], tfin.at[0, lo_rows], r1s.at[6], r1r.at[6], first(1))
    v = total(qm)
    tot[1] = v[256:512]
    t_m[0:256, :] = v[0:256].astype(BF)
    send(t_m.at[hi_rows], tfin.at[1, hi_rows], r1s.at[7], r1r.at[7], first(3))

    got(brecv.at[pl.ds(0, 7)], k1r)
    bsum[...] = jnp.sum(brecv[...], axis=0)
    ball[z] = bsum[...]
    to_head(lambda k: copy(bsum, ball.at[z], k2s, k2r, at_head(k)))

    mine_w = total(q)
    got(tbuf_p, r1r.at[4])
    t_p[0:256, :] = (tot[0] + tbuf_p[...].astype(F32)).astype(BF)
    send(t_p.at[hi_rows], tfin.at[0, hi_rows], r2s.at[2], r2r.at[2], first(1))
    got(tbuf_m, r1r.at[5])
    t_m[256:512, :] = (tot[1] + tbuf_m[...].astype(F32)).astype(BF)
    send(t_m.at[lo_rows], tfin.at[1, lo_rows], r2s.at[3], r2r.at[3], first(3))

    got(gg_all.at[many], ggr)
    gg_ref[...] = jnp.sum(gg_all[...], axis=0)
    got(call_.at[pl.ds(0, 7)], c2r)
    for k in range(8):
        gc_ref[32 * k : 32 * k + 32, :] = call_[k]
    got(rt_all.at[many], rtr)
    gr_ref[...] = jnp.sum(rt_all[...], axis=0)[:, 0:8]

    got(tfin.at[0, lo_rows], r1r.at[6])
    got(tfin.at[1, hi_rows], r1r.at[7])
    got(tfin.at[0, hi_rows], r2r.at[2])
    got(tfin.at[1, lo_rows], r2r.at[3])
    gw_ref[...] = jnp.transpose(mine_w + tfin[0].astype(F32) + tfin[1].astype(F32))
    got(ball.at[pl.ds(0, 7)], k2r)
    for k in range(8):
        gb_ref[32 * k : 32 * k + 32, :] = ball[k]

    def left(ref, sem):
        copy(ref, ref, sem, sem, partner).wait_send()

    for d in sent:
        d.wait_send()
    for ref, sem in (
        (dec_all, des), (st_recv, a1s), (st_recv, a2s), (ad_recv, b1s), (ad_recv, b2s),
        (gg_all, ggs), (rt_all, rts),
    ):
        left(ref.at[many], sem)
    for ref, sem in ((stat_all, sts), (crecv, c1s), (call_, c2s), (brecv, k1s), (ball, k2s)):
        left(ref.at[pl.ds(0, 7)], sem)


def on_device(
    inputs, gates, b_proj, c_proj, step_size, decay_rate, norm_gain, out_weight, grad_out
):
    V = pltpu.VMEM
    dma = pltpu.SemaphoreType.DMA
    scratch = [
        V((8, 256, 512), BF), V((2, 4, 4, 128, 512), BF),
        V((1, 1, 512), F32), V((32, 1, 512), F32),
        V((128, 512), F32), V((32, 8, 256), F32), V((32, 8, 256), F32), V((128, 512), F32),
        V((128, 512), F32), V((32, 8, 256), F32), V((32, 8, 256), F32), V((128, 512), F32),
        V((2, 256), F32), V((8, 2, 256), F32),
        V((4, 4, 512, 128), F32), V((4, 4, 512, 128), BF), V((4, 4, 512, 128), BF),
        V((4, 512, 128), BF), V((4, 512, 128), BF), V((4, 512, 128), BF),
        V((2, 512, 128), BF), V((2, 512, 128), BF), V((2, 4, 512, 128), BF),
        V((2, 256, 128), F32), V((512, 128), BF), V((512, 128), BF), V((512, 128), BF),
        V((256, 128), BF), V((256, 128), BF), V((2, 512, 128), BF),
        V((8, 32, 128), F32), V((8, 32, 128), F32), V((32, 128), F32), V((8, 32, 128), F32),
        V((8, 32, 128), F32), V((8, 32, 128), F32), V((32, 128), F32), V((8, 32, 128), F32),
        V((1, 1, 512), F32), V((32, 1, 512), F32), V((1, 1, 128), F32), V((32, 1, 128), F32),
        V((8, 128), F32), V((8, 256), F32), V((256, 128), F32), V((256, 128), F32),
        V((256, 512), F32), V((256, 512), F32), V((512, 512), BF),
        V((256, 256), F32), V((256, 256), F32),
        V((2, 128, 512), BF), V((2, 128, 1024), BF),
        V((256, 512), F32), V((256, 512), F32), V((256, 512), F32),
        V((256, 512), BF), V((512, 256), BF),
        V((256, 512), BF), V((256, 512), BF), V((512, 512), BF), V((256, 1024), BF),
        V((256, 128), F32), V((256, 256), F32), V((256, 128), F32), V((8, 256), F32),
        V((256, 512), F32), V((2, 256, 512), BF), V((256, 1024), F32),
        dma((2, 4, 2)), dma((2, 4, 2)), dma((4,)), dma((4,)), dma((4,)), dma((4,)),
        dma((5,)), dma((5,)),
        dma, dma, dma, dma, dma, dma, dma, dma, dma, dma, dma, dma,
        dma((4,)), dma((4,)), dma((8,)), dma((8,)), dma((4,)), dma((4,)),
        dma, dma, dma, dma, dma, dma, dma, dma, dma, dma, dma, dma,
    ]
    outs = (
        jax.ShapeDtypeStruct((256, 512), BF),
        jax.ShapeDtypeStruct((256, 512), BF),
        jax.ShapeDtypeStruct((256, 128), F32),
        jax.ShapeDtypeStruct((256, 128), F32),
        jax.ShapeDtypeStruct((8, 256), F32),
        jax.ShapeDtypeStruct((1, 8), F32),
        jax.ShapeDtypeStruct((1, 512), F32),
        jax.ShapeDtypeStruct((128, 512), F32),
    )
    spec = pl.BlockSpec(memory_space=pltpu.VMEM)
    gx, gz, gb, gc, gs, gr, gg, gw = pl.pallas_call(
        kernel,
        out_shape=outs,
        in_specs=[spec] * 9,
        out_specs=[spec] * 8,
        scratch_shapes=scratch,
        compiler_params=pltpu.CompilerParams(
            collective_id=0, has_side_effects=True, vmem_limit_bytes=60 * 1024 * 1024
        ),
    )(
        inputs, gates, b_proj, c_proj, step_size, decay_rate.reshape(1, 8),
        norm_gain.reshape(1, 512), out_weight, grad_out,
    )
    return gx, gz, gb, gc, gs, gr.reshape(8), gg.reshape(512), gw


def solution(mesh):
    split = Mesh(
        mesh.devices.reshape(4, 4, 2, mesh.shape["head"]), ("seq_0", "seq_1", "seq_2", "head")
    )
    return jax.shard_map(
        on_device,
        mesh=split,
        in_specs=(
            P(SEQ, "head"), P(SEQ, "head"), P(SEQ, None), P(SEQ, None), P("head", SEQ),
            P("head"), P("head"), P(SEQ, "head"), P(SEQ, "head"),
        ),
        out_specs=(
            P(SEQ, "head"), P(SEQ, "head"), P(SEQ, None), P(SEQ, None), P("head", SEQ),
            P("head"), P("head"), P(SEQ, "head"),
        ),
        check_vma=False,
    )
```

time: 470 us -> 84.8 us (0.18); the launches traced: 464 us -> 84.6 us
  matrix products: 116 us -> 0 us
  waiting for transfers between devices: 116 us -> 0 us
  other arithmetic: 78.1 us -> 0 us
  Pallas kernels: 0 us -> 77.4 us
  blocking collectives: 46.8 us -> 0 us
  local copies, waits for them, and re-layouts: 50.1 us -> 6.49 us
  starting transfers between devices: 31 us -> 0 us
  between operations: 15.8 us -> 0.66 us
  loops' own time: 11.2 us -> 0 us
    dot_general x93 -> x0, matrix products: 116 us -> none  [the longest x65 69.1 us: dot_high(): jnp.dot(left, right, precision=lax.Precision.HIGHEST, preferred_element_t...]
    pallas_call x0 -> x1, Pallas kernels: none -> 77.4 us  [on_device(): pl.pallas_call(kernel, out_shape=outs, in_specs=[spec] * 9, out_specs=[sp...]
    all_gather x5 -> x0, waiting for transfers between devices: 58.4 us -> none  [the longest x4 56.5 us: entering(): pieces = jax.tree.map(lambda part: lax.all_gather(part, axis), so_far)]
    all_to_all x4 -> x0, waiting for transfers between devices: 56.5 us -> none  [copy_for_each(): lax.all_to_all(jnp.broadcast_to(x[None], (peers, *x.shape)), axis, 0, 0,...]
    all_to_all x4 -> x0, starting transfers between devices: 30.6 us -> none  [copy_for_each(): lax.all_to_all(jnp.broadcast_to(x[None], (peers, *x.shape)), axis, 0, 0,...]
    mul x29 -> x0, other arithmetic: 25 us -> none  [the longest x16 21.6 us: decay_table(): logs = -jnp.cumsum(rate * step)]
    all_gather x4 -> x0, blocking collectives: 24.4 us -> none  [entering(): pieces = jax.tree.map(lambda part: lax.all_gather(part, axis), so_far)]
    reduce_sum x14 -> x0, other arithmetic: 20.5 us -> none  [the longest x8 15.1 us: span_backward(): rate_part = -jnp.sum(step * log_grad)]
  transfers between devices with their start and end apart: 10 -> 0, of which waited for: 7 -> 0; matrix products, arithmetic and copies ran while one was open for 48% -> 0% of each run, Pallas kernels for 0% -> 0%
where the time goes in v1:
time: 84.8 us; the launch traced here: 84.6 us
  Pallas kernels  77.4 us (91%)
  local copies, waits for them, and re-layouts  6.49 us (8%)
    pallas_call x1, Pallas kernels, on_device(): pl.pallas_call(kernel, out_shape=outs, in_specs=[spec] * 9, out_specs=[sp...  77.4 us
    unnamed x22, local copies, waits for them, and re-layouts  6.49 us

profile of v1, /device:TPU:1, one launch (start us, length us, event | category | flops | bytes accessed | tf_op | source)
XLA Modules:
  0.0 84.6 jit_solution(1382728968610376181)
XLA Ops:
  0.6 77.4 %shard_map.152 = (bf16[256,512]{1,0:T(8,128)(2,1)}, bf16[256,512]{1,0:T(8,128)(2,1)}, f32[256,128]{1,0:T(8,128)}, f32[256,128]{1,0:T(8,128)}, f32[8,256]{1,0:T(8...) custom-call(bf16[256,512]{1,0:T(8,128)(2,1)} %x_ref.1, bf16[256,512]{1,0:T(8,128)(2,1)} %z_ref.1, ...), custom_call_target="tpu_custom_call" | custom-call | tf_op jit(solution)/shard_map/pallas_call | solution.py:637
  78.1 0.0 copy-start.1
  78.1 1.7 %copy.25 = bf16[256,512]{1,0:T(8,128)(2,1)} copy(bf16[256,512]{1,0:T(8,128)(2,1)} %get-tuple-element.32) | data formatting | bytes 524288
  79.8 0.0 copy-done.1
  79.8 0.0 copy-start.3
  79.8 0.0 copy-start.2
  79.8 0.7 copy.26
  80.5 0.3 copy-done.3
  80.8 0.0 copy-start
  80.8 0.7 copy.27
  81.5 0.0 copy-done.2
  81.5 0.0 copy-start.4
  81.5 0.7 copy.28
  82.1 0.0 copy-done.4
  82.2 0.0 copy-start.6
  82.2 0.0 copy-start.5
  82.2 0.6 copy.29
  82.8 0.0 copy-done.6
  82.8 0.5 copy.30
  83.3 0.0 copy-done.5
  83.3 0.6 copy.31
  83.9 0.0 copy-done
  83.9 0.7 copy.32
Async XLA Ops:
  78.1 1.7 %copy-start.1 = (bf16[256,512]{1,0:T(8,128)(2,1)S(1)}, bf16[256,512]{1,0:T(8,128)(2,1)}, u32[]{:S(2)}) copy-start(bf16[256,512]{1,0:T(8,128)(2,1)} %get-tuple-element.33) | copy-start | bytes 786436
  79.8 1.0 %copy-start.3 = (f32[256,128]{1,0:T(8,128)S(1)}, f32[256,128]{1,0:T(8,128)}, u32[]{:S(2)}) copy-start(f32[256,128]{1,0:T(8,128)} %get-tuple-element.34) | copy-start | bytes 393220
  79.8 1.7 %copy-start.2 = (f32[256,128]{1,0:T(8,128)S(1)}, f32[256,128]{1,0:T(8,128)}, u32[]{:S(2)}) copy-start(f32[256,128]{1,0:T(8,128)} %get-tuple-element.35) | copy-start | bytes 393220
  80.8 3.1 %copy-start = (f32[128,512]{1,0:T(8,128)S(1)}, f32[128,512]{1,0:T(8,128)}, u32[]{:S(2)}) copy-start(f32[128,512]{1,0:T(8,128)} %get-tuple-element.39) | copy-start | bytes 786436
  81.5 0.7 copy-start.4
  82.2 0.6 copy-start.6
  82.2 1.1 %copy-start.5 = (f32[1,512]{1,0:T(1,128)S(1)}, f32[1,512]{1,0:T(1,128)}, u32[]{:S(2)}) copy-start(f32[1,512]{1,0:T(1,128)} %get-tuple-element.22) | copy-start | bytes 6148

commit v2 on v1

v2 whole, which is shorter than its diff:
```python
import jax
import jax.numpy as jnp
from jax import lax
from jax.experimental import pallas as pl
from jax.experimental.pallas import tpu as pltpu
from jax.sharding import Mesh
from jax.sharding import PartitionSpec as P

SEQ = ("seq_0", "seq_1", "seq_2")
EPSILON = 1e-05
MESH = pl.DeviceIdType.MESH
BF = jnp.bfloat16
F32 = jnp.float32


def mm(a, b):
    return jnp.dot(a, b, preferred_element_type=F32)


def nt(a, b):
    return lax.dot_general(a, b, (((1,), (1,)), ((), ())), preferred_element_type=F32)


def split2(v):
    hi = v.astype(BF)
    return hi, (v - hi.astype(F32)).astype(BF)


def split3(v):
    hi = v.astype(BF)
    rest = v - hi.astype(F32)
    mid = rest.astype(BF)
    return hi, mid, (rest - mid.astype(F32)).astype(BF)


def lanes(*parts):
    return jnp.concatenate(parts, axis=1)


def rows(*parts):
    return jnp.concatenate(parts, axis=0)


ORDER = (2, 1, 3, 0)


def kernel(
    x_hbm, z_hbm, b_hbm, c_hbm, step_hbm, rate_hbm, gain_hbm, w_hbm, g_hbm,
    gx_hbm, gz_hbm, gb_hbm, gc_hbm, gs_hbm, gr_hbm, gg_hbm, gw_hbm,
    gx_ref, gz_ref, gb_ref, gc_ref, gs_ref, gr_ref, gg_ref, gw_ref, outs,
    x_ref, z_ref, b_ref, c_ref, step_ref, rate_ref, gain_ref, w_ref, g_ref,
    gfull, wbuf, dec_src, dec_all, st_send, st_recv, st_pref, st_in,
    ad_send, ad_recv, ad_pref, ad_in, sq_src, sq_all, cr_src, cr_all,
    pt_own, pt_send, pt_recv, rs_o, rs_p, rs_m, buf_p, buf_m, fin,
    tot, t_o, t_p, t_m, tbuf_p, tbuf_m, tfin,
    cpart, crecv, csum, call_, bpart, brecv, bsum, ball,
    gg_src, gg_all, rt_src, rt_all,
    rate_c, lg, lgt, stept, fr, stl, xs2, sc, sct, mix_t, mix_b, ybuf, ycs, gn,
    ubuf, silb, ydb, nb, ntr, ehi, elo, ef2, rprod, colst, ws, qcol, rowp, gxi, mixw, pprod,
    ins, zs, zr, w1s, w1r, w2s, w2r, wfs, wfr, wds, wdr, des, der, a1s, a1r, a2s, a2r,
    b1s, b1r, b2s, b2r, sqs, sqr, crs, crr, d0s, d0r, r1s, r1r, r2s, r2r,
    c1s, c1r, c2s, c2r, k1s, k1r, k2s, k2r, ggs, ggr, rts, rtr,
):
    y = lax.axis_index("seq_0")
    x = lax.axis_index("seq_1")
    c = lax.axis_index("seq_2")
    z = lax.axis_index("head")
    me = (y * 4 + x) * 2 + c
    oc = 1 - c
    q = x * oc + y * c
    p = y * oc + x * c
    rem, div = lax.rem, lax.div

    def at_seq(k):
        return (div(k, 8), rem(div(k, 2), 4), rem(k, 2), z)

    def at_head(k):
        return (y, x, c, k)

    def first(d):
        return (rem(y + d * c, 4), rem(x + d * oc, 4), c, z)

    def second(d):
        return (rem(y + d * oc, 4), rem(x + d * c, 4), c, z)

    partner = (y, x, oc, z)

    def copy(src, dst, ssem, rsem, dev):
        return pltpu.make_async_remote_copy(
            src_ref=src, dst_ref=dst, send_sem=ssem, recv_sem=rsem,
            device_id=dev, device_id_type=MESH,
        )

    def got(ref, sem):
        copy(ref, ref, sem, sem, partner).wait_recv()

    sent, stored = [], []

    def store(src, dst):
        one = pltpu.make_async_copy(src, dst, outs.at[len(stored)])
        one.start()
        stored.append(one)

    def send(src, dst, ssem, rsem, dev):
        d = copy(src, dst, ssem, rsem, dev)
        d.start()
        sent.append(d)

    def to_seq(make):
        def one(d, carry):
            make(rem(me + d, 32)).start()
            return carry

        lax.fori_loop(1, 32, one, 0)

    def to_head(make):
        for d in (4, 3, 5, 2, 6, 1, 7):
            make(rem(z + d, 8)).start()

    barrier = pltpu.get_barrier_semaphore()
    for d in (4, 3, 5, 2, 6, 1, 7):
        pl.semaphore_signal(barrier, inc=1, device_id=at_head(rem(z + d, 8)), device_id_type=MESH)

    def greet(d, carry):
        pl.semaphore_signal(barrier, inc=1, device_id=at_seq(rem(me + d, 32)), device_id_type=MESH)
        return carry

    lax.fori_loop(1, 32, greet, 0)
    fetches = [
        pltpu.make_async_copy(src, dst, ins.at[i])
        for i, (src, dst) in enumerate((
            (step_hbm, step_ref), (rate_hbm, rate_ref), (gain_hbm, gain_ref), (b_hbm, b_ref),
            (x_hbm, x_ref), (c_hbm, c_ref), (g_hbm, g_ref), (w_hbm, w_ref), (z_hbm, z_ref),
        ))
    ]
    for f in fetches:
        f.start()
    for f in fetches[:4]:
        f.wait()

    i8 = lax.broadcasted_iota(jnp.int32, (8, 8), 0)
    j8 = lax.broadcasted_iota(jnp.int32, (8, 8), 1)
    rate = jnp.sum(jnp.where(i8 == j8, jnp.broadcast_to(rate_ref[...], (8, 8)), 0.0), axis=1, keepdims=True)
    rate_c[...] = jnp.broadcast_to(rate, (8, 128))
    step = step_ref[...]
    ia = lax.broadcasted_iota(jnp.int32, (256, 256), 0)
    ib = lax.broadcasted_iota(jnp.int32, (256, 256), 1)
    tri_u = jnp.where(ia <= ib, 1.0, 0.0).astype(BF)
    v1, v2, v3 = split3(rate * step)
    logs = -(mm(v1, tri_u) + mm(v2, tri_u) + mm(v3, tri_u))
    lg[...] = logs
    logs_t = jnp.transpose(logs)
    step_t = jnp.transpose(step)
    lgt[:, 0:8] = logs_t
    stept[:, 0:8] = step_t
    e8 = jnp.where(
        lax.broadcasted_iota(jnp.int32, (8, 512), 0)
        == lax.broadcasted_iota(jnp.int32, (8, 512), 1) // 64, 1.0, 0.0,
    ).astype(BF)

    def spread_heads(v):
        a1, a2, a3 = split3(v)
        return mm(a1, e8) + mm(a2, e8) + mm(a3, e8)

    fr[...] = spread_heads(jnp.exp(logs_t))
    stl[...] = spread_heads(step_t * jnp.exp(logs_t[255:256, :] - logs_t))
    dec_src[0] = fr[255:256, :]
    dec_all[me] = fr[255:256, :]
    bt = b_ref[...].T
    fetches[4].wait()
    for r in range(4):
        rs = slice(64 * r, 64 * r + 64)
        hi, lo = split2(x_ref[rs, :].astype(F32) * stl[rs, :])
        xs2[rs, :] = hi
        xs2[64 * r + 256 : 64 * r + 320, :] = lo
    st_send[...] = mm(lanes(bt, bt), xs2[...])
    for f in fetches[5:]:
        f.wait()

    pl.semaphore_wait(barrier, 38)

    qm, qp, q2 = rem(q + 3, 4), rem(q + 1, 4), rem(q + 2, 4)
    pm, pp, p2 = rem(p + 3, 4), rem(p + 1, 4), rem(p + 2, 4)
    top, low = pl.ds(0, 64), pl.ds(64, 64)
    both_z, both_4 = ((0, 1), (1, 7)), ((0, 1), (1, 3))
    for k in range(2):
        rk = pl.ds(128 * k, 128)
        for side, d in both_z:
            send(g_ref.at[rk], gfull.at[z, rk], zs.at[side, 0, k], zr.at[side, 0, k], at_head(rem(z + d, 8)))
    for side, d in both_4:
        send(w_ref, wbuf.at[c, p, q], w1s.at[side], w1r.at[side], first(d))
    to_seq(lambda k: copy(dec_src.at[0], dec_all.at[me], des, der, at_seq(k)))

    def slab(ref, k):
        return ref.at[
            pl.ds(pl.multiple_of(8 * div(k, 2), 8), 8),
            pl.ds(pl.multiple_of(256 * rem(k, 2), 256), 256),
        ]

    to_seq(lambda k: copy(slab(st_send, k), st_recv.at[me], a1s, a1r, at_seq(k)))
    for side, d in both_4:
        send(w_ref, wbuf.at[c, p, q], w2s.at[side, 0], w2r.at[side, 0], second(d))
    st_recv[me] = slab(st_send, me)[...]
    gfull[z] = g_ref[...]
    wbuf[c, p, q] = w_ref[...]

    iota_i = lax.broadcasted_iota(jnp.int32, (64, 256), 0)
    iota_j = lax.broadcasted_iota(jnp.int32, (64, 256), 1)
    ct = c_ref[...].T
    raw = mm(c_ref[...], bt)
    for r in range(4):
        rs = slice(64 * r, 64 * r + 64)
        sc[rs, :] = jnp.where(iota_i + 64 * r >= iota_j, raw[rs, :], 0.0)
    sct[...] = mm(b_ref[...], ct)

    got(wbuf.at[c, p, qm], w1r.at[0])
    send(wbuf.at[c, p, qm, top], wbuf.at[c, p, qm, top], w1s.at[2], w1r.at[2], first(1))
    for side, d in both_4:
        send(wbuf.at[c, p, qm], wbuf.at[c, p, qm], w2s.at[side, 1], w2r.at[side, 1], second(d))
    got(wbuf.at[c, p, qp], w1r.at[1])
    send(wbuf.at[c, p, qp, low], wbuf.at[c, p, qp, low], w1s.at[3], w1r.at[3], first(3))
    for side, d in both_4:
        send(wbuf.at[c, p, qp], wbuf.at[c, p, qp], w2s.at[side, 2], w2r.at[side, 2], second(d))

    half = lax.broadcasted_iota(jnp.int32, (1, 128), 1)
    keep = (
        jnp.where(half < 64, 1.0, 0.0).astype(BF),
        jnp.where(half < 64, 0.0, 1.0).astype(BF),
    )

    def inside(hp):
        ls = slice(128 * hp, 128 * hp + 128)
        mt, mb = mix_t.at[hp % 2], mix_b.at[hp % 2]
        xp = x_ref[:, ls]
        x0, x1 = xp * keep[0], xp * keep[1]
        for k in range(2):
            h = 2 * hp + k
            for r in range(4):
                rs = slice(64 * r, 64 * r + 64)
                wd = 128 if r < 2 else 256
                t = jnp.exp(jnp.minimum(lgt[rs, h : h + 1] - lg[h : h + 1, 0:wd], 0.0))
                hi, lo = split2(t * (sc[rs, 0:wd] * step_ref[h : h + 1, 0:wd]))
                dst = mt if r < 2 else mb
                rr = slice(64 * (r % 2), 64 * (r % 2) + 64)
                dst[rr, 2 * k * wd : (2 * k + 1) * wd] = hi
                dst[rr, (2 * k + 1) * wd : (2 * k + 2) * wd] = lo
        ybuf[0:128, ls] = mm(mt[...], rows(x0[0:128], x0[0:128], x1[0:128], x1[0:128]))
        ybuf[128:256, ls] = mm(mb[...], rows(x0, x0, x1, x1))

    def z_block(side, j):
        return rem(z + 8 - j, 8) if side == 0 else rem(z + j, 8)

    def z_forward(j):
        for k in range(2):
            rk = pl.ds(128 * k, 128)
            for side, d in both_z:
                blk = gfull.at[z_block(side, j), rk]
                got(blk, zr.at[side, j - 1, k])
                if j < 3 or k == side:
                    send(blk, blk, zs.at[side, j, k], zr.at[side, j, k], at_head(rem(z + d, 8)))

    spots = (q, qm, qp, q2, q2)

    def w_forward(slot):
        for side, row in ((0, pm), (1, pp)):
            if slot < 3:
                blk = wbuf.at[c, row, spots[slot]]
                part = blk.at[top if side == 0 else low]
                on = True
            else:
                blk = part = wbuf.at[c, row, q2, top if slot == 3 else low]
                on = slot == 3 + side
            got(blk, w2r.at[side, slot])
            if on:
                n = min(slot, 3)
                send(part, part, wfs.at[side, n], wfr.at[side, n], second(1 if side == 0 else 3))

    def w_second_of_opposite():
        for n, piece in ((0, top), (1, low)):
            blk = wbuf.at[c, p, q2, piece]
            got(blk, w1r.at[2 + n])
            for side, d in both_4:
                send(blk, blk, w2s.at[side, 3 + n], w2r.at[side, 3 + n], second(d))

    def to_partner(n, i2):
        send(wbuf.at[c, i2], wbuf.at[c, i2], wds.at[n], wdr.at[n], partner)

    def scan(recv, pref, back):
        s = jnp.zeros((8, 256), F32)
        for k in reversed(range(32)) if back else range(32):
            pref[k] = s
            s = s * dec_all[k, :, pl.ds(pl.multiple_of(256 * c, 256), 256)] + recv[k]

    many = pl.ds(0, 31)

    inside(0)
    w_forward(0)
    w_second_of_opposite()
    to_partner(0, p)
    inside(1)
    z_forward(1)
    got(dec_all.at[many], der)
    got(st_recv.at[many], a1r)
    scan(st_recv, st_pref, False)
    to_seq(lambda k: copy(st_pref.at[k], slab(st_in, me), a2s, a2r, at_seq(k)))
    slab(st_in, me)[...] = st_pref[me]
    w_forward(1)
    w_forward(2)
    inside(2)
    inside(3)
    w_forward(3)
    w_forward(4)
    to_partner(1, pm)
    to_partner(2, pp)
    z_forward(2)

    got(st_recv.at[many], a2r)
    s_hi, s_lo = split2(st_in[...])
    cc = lanes(c_ref[...], c_ref[...])
    gain = gain_ref[...]

    def folded(v):
        return v[:, 0:128] + v[:, 128:256] + v[:, 256:384] + v[:, 384:512]

    for r in range(4):
        rs = slice(64 * r, 64 * r + 64)
        v = fr[rs, :] * mm(cc[rs, :], rows(s_hi, s_lo))
        ycs[rs, :] = v
        ybuf[rs, :] = ybuf[rs, :] + v
    for r in range(8):
        rs = slice(32 * r, 32 * r + 32)
        zf = z_ref[rs, :].astype(F32)
        yv = ybuf[rs, :]
        s = 1.0 / (1.0 + jnp.exp(-zf))
        sil = zf * s
        u = yv * sil
        ubuf[rs, :] = u
        silb[rs, :] = sil
        ydb[rs, :] = yv * s * (1.0 + zf * (1.0 - s))
        pprod[rs, 0:128] = folded(u * u)
    sq = jnp.sum(jnp.transpose(pprod[:, 0:128]), axis=0, keepdims=True)
    sq_src[0] = sq
    sq_all[z] = sq
    to_head(lambda k: copy(sq_src.at[0], sq_all.at[z], sqs, sqr, at_head(k)))

    for n in range(4):
        i1 = (q, qm, qp, q2)[n]
        got(wbuf.at[c, p2, i1, top], wfr.at[0, n])
        got(wbuf.at[c, p2, i1, low], wfr.at[1, n])
    to_partner(3, p2)
    z_forward(3)
    for n in range(4):
        got(wbuf.at[oc, p], wdr.at[n])

    gn[...] = jnp.zeros((256, 512), F32)

    def add_block(h):
        yy, xx = div(h, 2), 2 * rem(h, 2)
        rhs = rows(wbuf[0, yy, xx], wbuf[1, xx, yy], wbuf[0, yy, xx + 1], wbuf[1, xx + 1, yy])
        gn[...] = gn[...] + mm(gfull[h], rhs)

    def one_block(d, carry):
        add_block(rem(z + 5 + d, 8))
        return carry

    lax.fori_loop(0, 7, one_block, 0)
    for side in range(2):
        got(gfull.at[z_block(side, 4), pl.ds(128 * side, 128)], zr.at[side, 3, side])
    add_block(rem(z + 4, 8))
    for r in range(8):
        rs = slice(32 * r, 32 * r + 32)
        pprod[rs, 128:256] = folded(gn[rs, :] * gain * ubuf[rs, :])
    cr = jnp.sum(jnp.transpose(pprod[:, 128:256]), axis=0, keepdims=True)
    cr_src[0] = cr
    cr_all[z] = cr
    to_head(lambda k: copy(cr_src.at[0], cr_all.at[z], crs, crr, at_head(k)))

    seven = pl.ds(0, 7)
    got(sq_all.at[seven], sqr)
    inv_row = lax.rsqrt(jnp.sum(sq_all[...], axis=0) / 4096.0 + EPSILON)
    zero7 = jnp.zeros((7, 256), F32)
    colst[:, 0:8] = jnp.transpose(rows(inv_row, zero7))
    gg_acc = jnp.zeros((8, 512), F32)
    for r in range(8):
        rs = slice(32 * r, 32 * r + 32)
        ui = ubuf[rs, :] * colst[rs, 0:1]
        nb[rs, :] = (ui * gain).astype(BF)
        gg_acc = gg_acc + jnp.sum((gn[rs, :] * ui).reshape(4, 8, 512), axis=0)
    ntr[...] = nb[...].T

    for n in range(4):
        i2 = rem(q + ORDER[n], 4)

        def one_chip(i1, carry, i2=i2):
            yy, xx = i2 * c + i1 * oc, i1 * c + i2 * oc
            blk = 2 * yy + div(xx, 2)
            base = rem(xx, 2) * 256
            mine = gfull[blk, :, pl.ds(pl.multiple_of(base + 128 * c, 128), 128)]
            other = gfull[blk, :, pl.ds(pl.multiple_of(base + 128 * oc, 128), 128)]
            both = mm(ntr[...], lanes(mine, other))
            pt_own[yy * oc + xx * c, xx * oc + yy * c] = both[:, 0:128]
            pt_send[i2, i1] = both[:, 128:256].astype(BF)
            return carry

        lax.fori_loop(0, 4, one_chip, 0)
        send(pt_send.at[i2], pt_recv.at[i2], d0s.at[n], d0r.at[n], partner)

    gg_src[0] = jnp.sum(gg_acc, axis=0, keepdims=True)
    gg_all[me] = gg_src[0]
    ab, cd = pl.ds(0, 2), pl.ds(2, 2)
    got(pt_recv.at[p2], d0r.at[0])
    for i in range(4):
        rs_o[i] = (pt_own[p2, i] + pt_recv[p2, i].astype(F32)).astype(BF)
    send(rs_o.at[ab], buf_p, r1s.at[0], r1r.at[0], second(1))
    send(rs_o.at[cd], buf_m, r1s.at[1], r1r.at[1], second(3))

    got(cr_all.at[seven], crr)
    coef_row = inv_row * inv_row * (jnp.sum(cr_all[...], axis=0) / 4096.0)
    colst[:, 8:16] = jnp.transpose(rows(coef_row, zero7))
    for r in range(8):
        rs = slice(32 * r, 32 * r + 32)
        gu = colst[rs, 0:1] * (gn[rs, :] * gain - ubuf[rs, :] * colst[rs, 8:9])
        gz_ref[rs, :] = (gu * ydb[rs, :]).astype(BF)
        e = gu * silb[rs, :]
        hi, lo = split2(e)
        ehi[rs, :] = hi
        elo[rs, :] = lo
        hi, lo = split2(e * fr[rs, :])
        ef2[rs, :] = hi
        ef2[256 + 32 * r : 288 + 32 * r, :] = lo
        hi, lo = split2(e * ycs[rs, :])
        rprod[rs, 0:512] = hi
        rprod[rs, 512:1024] = lo
    ad_send[...] = mm(lanes(ct, ct), ef2[...])
    to_seq(lambda k: copy(slab(ad_send, k), ad_recv.at[me], b1s, b1r, at_seq(k)))
    ad_recv[me] = slab(ad_send, me)[...]
    store(gz_ref, gz_hbm)
    to_seq(lambda k: copy(gg_src.at[0], gg_all.at[me], ggs, ggr, at_seq(k)))

    got(pt_recv.at[pp], d0r.at[1])
    for i in range(4):
        v = pt_own[pp, i] + pt_recv[pp, i].astype(F32)
        if i < 2:
            pt_own[pp, i] = v
        else:
            rs_p[i] = v.astype(BF)
    send(rs_p.at[cd], fin.at[0, cd], r1s.at[2], r1r.at[2], second(1))
    got(pt_recv.at[pm], d0r.at[2])
    for i in range(4):
        v = pt_own[pm, i] + pt_recv[pm, i].astype(F32)
        if i < 2:
            rs_m[i] = v.astype(BF)
        else:
            pt_own[pm, i] = v
    send(rs_m.at[ab], fin.at[1, ab], r1s.at[3], r1r.at[3], second(3))

    mask_t = (iota_j >= iota_i, iota_j >= iota_i + 64)
    mask_b = (iota_j[:, 0:128] >= iota_i[:, 0:128], iota_j[:, 0:128] >= iota_i[:, 0:128] + 64)

    def inside_back(hp):
        ls = slice(128 * hp, 128 * hp + 128)
        mw = mixw.at[hp % 2]
        xp = x_ref[:, ls]
        eh, el = ehi[:, ls], elo[:, ls]
        e2 = lanes(eh, el)
        for k in range(2):
            h = 2 * hp + k
            xk = xp * keep[k]
            x2 = lanes(xk, xk)
            inner_t = nt(x2[0:128], e2)
            inner_b = nt(x2[128:256], e2[128:256])
            racc_l = jnp.zeros((1, 128), F32)
            racc_r = jnp.zeros((1, 128), F32)
            for r in range(4):
                rs = slice(64 * r, 64 * r + 64)
                rr = slice(64 * (r % 2), 64 * (r % 2) + 64)
                cs = slice(0, 256) if r < 2 else slice(128, 256)
                t = jnp.exp(jnp.minimum(lg[h : h + 1, cs] - lgt[rs, h : h + 1], 0.0))
                tab = jnp.where(mask_t[r] if r < 2 else mask_b[r - 2], t, 0.0)
                inner = inner_t[rr] if r < 2 else inner_b[rr]
                st = sct[rs, cs]
                sj = stept[rs, h : h + 1]
                w = tab * inner
                sw = w * sj
                if r < 2:
                    mw[rr, 256 * k : 256 * k + 256] = (tab * st * sj).astype(BF)
                else:
                    mw[128 + 64 * (r - 2) : 192 + 64 * (r - 2), 128 * k : 128 * k + 128] = (tab * st * sj).astype(BF)
                qcol[rs, h : h + 1] = jnp.sum(w * st, axis=1, keepdims=True)
                if h == 0:
                    ws[rs, cs] = sw
                else:
                    ws[rs, cs] = ws[rs, cs] + sw
                rsum = jnp.sum(sw * st, axis=0, keepdims=True)
                if r < 2:
                    racc_l = racc_l + rsum[:, 0:128]
                    racc_r = racc_r + rsum[:, 128:256]
                else:
                    racc_r = racc_r + rsum
            rowp[h : h + 1, 0:128] = racc_l
            rowp[h : h + 1, 128:256] = racc_r
        em0, em1 = lanes(eh * keep[0], el * keep[0]), lanes(eh * keep[1], el * keep[1])
        v = mm(mw[0:128, :], rows(em0, em1))
        gxi[0:128, ls] = v[:, 0:128] + v[:, 128:256]
        v = mm(mw[128:256, 0:256], rows(em0[128:256], em1[128:256]))
        gxi[128:256, ls] = v[:, 0:128] + v[:, 128:256]

    for hp in range(4):
        inside_back(hp)

    got(ad_recv.at[many], b1r)
    scan(ad_recv, ad_pref, True)
    to_seq(lambda k: copy(ad_pref.at[k], slab(ad_in, me), b2s, b2r, at_seq(k)))
    slab(ad_in, me)[...] = ad_pref[me]

    got(buf_p, r1r.at[0])
    for i in range(2):
        rs_p[i] = (pt_own[pp, i] + buf_p[i].astype(F32)).astype(BF)
    send(rs_p.at[ab], fin.at[0, ab], r2s.at[0], r2r.at[0], second(1))
    got(buf_m, r1r.at[1])
    for i in range(2):
        rs_m[2 + i] = (pt_own[pm, 2 + i] + buf_m[i].astype(F32)).astype(BF)
    send(rs_m.at[cd], fin.at[1, cd], r2s.at[1], r2r.at[1], second(3))

    ws[128:256, 0:128] = jnp.zeros((128, 128), F32)
    w_hi, w_lo = split2(jnp.transpose(ws[...]))
    gq = mm(lanes(w_hi, w_lo), rows(b_ref[...], b_ref[...]))
    gq = gq + nt(lanes(ef2[0:256], ef2[256:512], ef2[0:256]), lanes(s_hi, s_hi, s_lo))
    for k in range(8):
        cpart[k] = gq[32 * k : 32 * k + 32]
    crecv[z] = cpart[z]
    to_head(lambda k: copy(cpart.at[k], crecv.at[z], c1s, c1r, at_head(k)))
    w_hi, w_lo = split2(ws[...])
    gk = mm(lanes(w_hi, w_lo), rows(c_ref[...], c_ref[...]))

    got(pt_recv.at[p], d0r.at[3])
    for i in range(4):
        pt_own[p, i] = pt_own[p, i] + pt_recv[p, i].astype(F32)
    e16 = lanes(e8, e8)
    rstate = nt(e16, rprod[...])

    got(ad_recv.at[many], b2r)
    a_hi, a_lo = split2(ad_in[...])
    gk = gk + nt(lanes(xs2[0:256], xs2[256:512], xs2[0:256]), lanes(a_hi, a_hi, a_lo))
    for k in range(8):
        bpart[k] = gk[32 * k : 32 * k + 32].astype(BF)
    brecv[z] = bpart[z]
    to_head(lambda k: copy(bpart.at[k], brecv.at[z], k1s, k1r, at_head(k)))
    got(crecv.at[seven], c1r)
    csum[...] = jnp.sum(crecv[...], axis=0)
    call_[z] = csum[...]
    to_head(lambda k: copy(csum, call_.at[z], c2s, c2r, at_head(k)))

    for r in range(4):
        rs = slice(64 * r, 64 * r + 64)
        ka = mm(lanes(b_ref[rs, :], b_ref[rs, :]), rows(a_hi, a_lo))
        gx_ref[rs, :] = (gxi[rs, :] + stl[rs, :] * ka).astype(BF)
        hi, lo = split2(x_ref[rs, :].astype(F32) * ka)
        pprod[rs, 0:512] = hi.astype(F32)
        pprod[rs, 512:1024] = lo.astype(F32)
    carr = nt(e16, pprod[...].astype(BF))
    store(gx_ref, gx_hbm)
    held = jnp.sum((ad_in[...] * st_in[...]).reshape(16, 8, 512), axis=0)
    h_hi, h_lo = split2(held)
    held8 = jnp.sum(nt(e16, lanes(h_hi, h_lo)), axis=1, keepdims=True)
    logs = lg[...]
    step = step_ref[...]
    rate = rate_c[:, 0:1]
    tail = jnp.exp(logs[:, 255:256] - logs)
    q_in = jnp.transpose(qcol[...])[0:8, :]
    tc = tail * carr
    q_terms = q_in + tc
    drive = rowp[...] + rstate - step * q_terms
    boundary = jnp.exp(logs[:, 255:256]) * held8 + jnp.sum(step * tc, axis=1, keepdims=True)
    tri_l = jnp.where(ia >= ib, 1.0, 0.0).astype(BF)
    v1, v2, v3 = split3(drive)
    log_grad = mm(v1, tri_l) + mm(v2, tri_l) + mm(v3, tri_l) + boundary
    gs_ref[...] = q_terms - rate * log_grad
    rp = -jnp.sum(step * log_grad, axis=1, keepdims=True)
    d0 = lax.broadcasted_iota(jnp.int32, (8, 128), 0)
    d1 = lax.broadcasted_iota(jnp.int32, (8, 128), 1)
    rt_src[0] = jnp.sum(jnp.where(d0 == d1, rp, 0.0), axis=0, keepdims=True)
    rt_all[me] = rt_src[0]
    to_seq(lambda k: copy(rt_src.at[0], rt_all.at[me], rts, rtr, at_seq(k)))
    store(gs_ref, gs_hbm)

    got(fin.at[0, cd], r1r.at[2])
    got(fin.at[1, ab], r1r.at[3])
    got(fin.at[0, ab], r2r.at[0])
    got(fin.at[1, cd], r2r.at[1])

    def total(i):
        return pt_own[p, i] + fin[0, i].astype(F32) + fin[1, i].astype(F32)

    hi_rows, lo_rows = pl.ds(0, 256), pl.ds(256, 256)
    t_o[...] = total(q2).astype(BF)
    send(t_o.at[hi_rows], tbuf_p, r1s.at[4], r1r.at[4], first(1))
    send(t_o.at[lo_rows], tbuf_m, r1s.at[5], r1r.at[5], first(3))
    v = total(qp)
    tot[0] = v[0:256]
    t_p[256:512, :] = v[256:512].astype(BF)
    send(t_p.at[lo_rows], tfin.at[0, lo_rows], r1s.at[6], r1r.at[6], first(1))
    v = total(qm)
    tot[1] = v[256:512]
    t_m[0:256, :] = v[0:256].astype(BF)
    send(t_m.at[hi_rows], tfin.at[1, hi_rows], r1s.at[7], r1r.at[7], first(3))

    got(brecv.at[seven], k1r)
    bsum[...] = jnp.sum(brecv[...].astype(F32), axis=0).astype(BF)
    ball[z] = bsum[...]
    to_head(lambda k: copy(bsum, ball.at[z], k2s, k2r, at_head(k)))

    mine_w = total(q)
    got(tbuf_p, r1r.at[4])
    t_p[0:256, :] = (tot[0] + tbuf_p[...].astype(F32)).astype(BF)
    send(t_p.at[hi_rows], tfin.at[0, hi_rows], r2s.at[2], r2r.at[2], first(1))
    got(tbuf_m, r1r.at[5])
    t_m[256:512, :] = (tot[1] + tbuf_m[...].astype(F32)).astype(BF)
    send(t_m.at[lo_rows], tfin.at[1, lo_rows], r2s.at[3], r2r.at[3], first(3))

    got(gg_all.at[many], ggr)
    gg_ref[...] = jnp.sum(gg_all[...], axis=0)
    store(gg_ref, gg_hbm)
    got(call_.at[seven], c2r)
    for k in range(8):
        gc_ref[32 * k : 32 * k + 32, :] = call_[k]
    store(gc_ref, gc_hbm)
    got(rt_all.at[many], rtr)
    gr_ref[...] = jnp.sum(rt_all[...], axis=0)[:, 0:8]
    store(gr_ref, gr_hbm)

    got(tfin.at[0, lo_rows], r1r.at[6])
    got(tfin.at[1, hi_rows], r1r.at[7])
    got(tfin.at[0, hi_rows], r2r.at[2])
    got(tfin.at[1, lo_rows], r2r.at[3])
    gw_ref[...] = jnp.transpose(mine_w + tfin[0].astype(F32) + tfin[1].astype(F32))
    store(gw_ref, gw_hbm)
    got(ball.at[seven], k2r)
    for k in range(8):
        gb_ref[32 * k : 32 * k + 32, :] = ball[k].astype(F32)
    store(gb_ref, gb_hbm)

    def left(ref, sem):
        copy(ref, ref, sem, sem, partner).wait_send()

    for d in sent:
        d.wait_send()
    for d in stored:
        d.wait()
    for ref, sem in (
        (dec_all, des), (st_recv, a1s), (st_recv, a2s), (ad_recv, b1s), (ad_recv, b2s),
        (gg_all, ggs), (rt_all, rts),
    ):
        left(ref.at[many], sem)
    for ref, sem in ((sq_all, sqs), (cr_all, crs), (crecv, c1s), (call_, c2s), (brecv, k1s), (ball, k2s)):
        left(ref.at[seven], sem)


def hand_over(*refs):
    took = [pltpu.make_async_copy(refs[i], refs[16 + i], refs[24].at[i]) for i in range(8)]
    gave = [pltpu.make_async_copy(refs[16 + i], refs[8 + i], refs[24].at[8 + i]) for i in range(8)]
    for one in took:
        one.start()
    for one, other in zip(took, gave):
        one.wait()
        other.start()
    for one in gave:
        one.wait()


def on_device(
    inputs, gates, b_proj, c_proj, step_size, decay_rate, norm_gain, out_weight, grad_out
):
    V = pltpu.VMEM
    dma = pltpu.SemaphoreType.DMA
    scratch = [
        V((256, 512), BF), V((256, 512), BF), V((256, 128), F32), V((256, 128), F32),
        V((8, 256), F32), V((1, 8), F32), V((1, 512), F32), V((128, 512), F32), dma((8,)),
        V((256, 512), BF), V((256, 512), BF), V((256, 128), BF), V((256, 128), BF),
        V((8, 256), F32), V((1, 8), F32), V((1, 512), F32), V((128, 512), BF), V((256, 512), BF),
        V((8, 256, 512), BF), V((2, 4, 4, 128, 512), BF),
        V((1, 1, 512), F32), V((32, 1, 512), F32),
        V((128, 512), F32), V((32, 8, 256), F32), V((32, 8, 256), F32), V((128, 512), F32),
        V((128, 512), F32), V((32, 8, 256), F32), V((32, 8, 256), F32), V((128, 512), F32),
        V((1, 1, 256), F32), V((8, 1, 256), F32), V((1, 1, 256), F32), V((8, 1, 256), F32),
        V((4, 4, 512, 128), F32), V((4, 4, 512, 128), BF), V((4, 4, 512, 128), BF),
        V((4, 512, 128), BF), V((4, 512, 128), BF), V((4, 512, 128), BF),
        V((2, 512, 128), BF), V((2, 512, 128), BF), V((2, 4, 512, 128), BF),
        V((2, 256, 128), F32), V((512, 128), BF), V((512, 128), BF), V((512, 128), BF),
        V((256, 128), BF), V((256, 128), BF), V((2, 512, 128), BF),
        V((8, 32, 128), F32), V((8, 32, 128), F32), V((32, 128), F32), V((8, 32, 128), F32),
        V((8, 32, 128), BF), V((8, 32, 128), BF), V((32, 128), BF), V((8, 32, 128), BF),
        V((1, 1, 512), F32), V((32, 1, 512), F32), V((1, 1, 128), F32), V((32, 1, 128), F32),
        V((8, 128), F32), V((8, 256), F32), V((256, 128), F32), V((256, 128), F32),
        V((256, 512), F32), V((256, 512), F32), V((512, 512), BF),
        V((256, 256), F32), V((256, 256), F32),
        V((2, 128, 512), BF), V((2, 128, 1024), BF),
        V((256, 512), F32), V((256, 512), F32), V((256, 512), F32),
        V((256, 512), F32), V((256, 512), F32), V((256, 512), F32),
        V((256, 512), BF), V((512, 256), BF),
        V((256, 512), BF), V((256, 512), BF), V((512, 512), BF), V((256, 1024), BF),
        V((256, 128), F32), V((256, 256), F32), V((256, 128), F32), V((8, 256), F32),
        V((256, 512), F32), V((2, 256, 512), BF), V((256, 1024), F32),
        dma((9,)), dma((2, 4, 2)), dma((2, 4, 2)), dma((4,)), dma((4,)), dma((2, 5)), dma((2, 5)),
        dma((2, 4)), dma((2, 4)), dma((4,)), dma((4,)),
        dma, dma, dma, dma, dma, dma, dma, dma, dma, dma, dma, dma, dma, dma,
        dma((4,)), dma((4,)), dma((8,)), dma((8,)), dma((4,)), dma((4,)),
        dma, dma, dma, dma, dma, dma, dma, dma, dma, dma, dma, dma,
    ]
    outs = (
        jax.ShapeDtypeStruct((256, 512), BF),
        jax.ShapeDtypeStruct((256, 512), BF),
        jax.ShapeDtypeStruct((256, 128), F32),
        jax.ShapeDtypeStruct((256, 128), F32),
        jax.ShapeDtypeStruct((8, 256), F32),
        jax.ShapeDtypeStruct((1, 8), F32),
        jax.ShapeDtypeStruct((1, 512), F32),
        jax.ShapeDtypeStruct((128, 512), F32),
    )
    far = pl.BlockSpec(memory_space=pltpu.HBM)
    results = pl.pallas_call(
        kernel,
        out_shape=outs,
        in_specs=[far] * 9,
        out_specs=[far] * 8,
        scratch_shapes=scratch,
        compiler_params=pltpu.CompilerParams(
            collective_id=0, has_side_effects=True, vmem_limit_bytes=60000000
        ),
    )(
        inputs, gates, b_proj, c_proj, step_size, decay_rate.reshape(1, 8),
        norm_gain.reshape(1, 512), out_weight, grad_out,
    )
    gx, gz, gb, gc, gs, gr, gg, gw = pl.pallas_call(
        hand_over,
        out_shape=outs,
        in_specs=[far] * 8,
        out_specs=[far] * 8,
        scratch_shapes=[V(o.shape, o.dtype) for o in outs] + [dma((16,))],
        compiler_params=pltpu.CompilerParams(vmem_limit_bytes=60000000),
    )(*results)
    return gx, gz, gb, gc, gs, gr.reshape(8), gg.reshape(512), gw


def solution(mesh):
    split = Mesh(
        mesh.devices.reshape(4, 4, 2, mesh.shape["head"]), ("seq_0", "seq_1", "seq_2", "head")
    )
    return jax.shard_map(
        on_device,
        mesh=split,
        in_specs=(
            P(SEQ, "head"), P(SEQ, "head"), P(SEQ, None), P(SEQ, None), P("head", SEQ),
            P("head"), P("head"), P(SEQ, "head"), P(SEQ, "head"),
        ),
        out_specs=(
            P(SEQ, "head"), P(SEQ, "head"), P(SEQ, None), P(SEQ, None), P("head", SEQ),
            P("head"), P("head"), P(SEQ, "head"),
        ),
        check_vma=False,
    )
```

time: 84.8 us -> 74 us (0.87)
  local copies, waits for them, and re-layouts: 6.49 us -> 0 us
  Pallas kernels: 77.4 us -> 73.2 us
    unnamed x22 -> x0, local copies, waits for them, and re-layouts: 6.49 us -> none
    pallas_call x1 -> x2, Pallas kernels: 77.4 us -> 73.2 us  [the longest x1 71.1 us: on_device(): pl.pallas_call(kernel, out_shape=outs, in_specs=[far] * 9, out_specs=[far...]
where the time goes in v2:
time: 74 us; the launch traced here: 73.8 us
  Pallas kernels  73.2 us (99%)
    pallas_call x1, Pallas kernels, on_device(): pl.pallas_call(kernel, out_shape=outs, in_specs=[far] * 9, out_specs=[far...  71.1 us
    pallas_call x1, Pallas kernels, on_device(): pl.pallas_call(hand_over, out_shape=outs, in_specs=[far] * 8, out_specs=[...  2.07 us

profile of v2, /device:TPU:1, one launch (start us, length us, event | category | flops | bytes accessed | tf_op | source)
XLA Modules:
  0.0 73.8 jit_solution(12226788413128195481)
XLA Ops:
  0.6 71.1 %shard_map.152 = (bf16[256,512]{1,0:T(8,128)(2,1)}, bf16[256,512]{1,0:T(8,128)(2,1)}, f32[256,128]{1,0:T(8,128)}, f32[256,128]{1,0:T(8,128)}, f32[8,256]{1,0:T(8...) custom-call(bf16[256,512]{1,0:T(8,128)(2,1)} %x_hbm.1, bf16[256,512]{1,0:T(8,128)(2,1)} %z_hbm.1, ...), custom_call_target="tpu_custom_call" | custom-call | tf_op jit(solution)/shard_map/pallas_call | solution.py:721
  71.8 2.1 %shard_map.153 = (bf16[256,512]{1,0:T(8,128)(2,1)}, bf16[256,512]{1,0:T(8,128)(2,1)}, f32[256,128]{1,0:T(8,128)}, f32[256,128]{1,0:T(8,128)}, f32[8,256]{1,0:T(8...) custom-call(bf16[256,512]{1,0:T(8,128)(2,1)} %get-tuple-element.24.refs_0_, ...), custom_call_target="tpu_custom_call" | custom-call | tf_op jit(solution)/shard_map/pallas_call | solution.py:734

commit v3 on v2

--- a/solution.py
+++ b/solution.py
@@ -49,15 +49,16 @@
     gx_hbm, gz_hbm, gb_hbm, gc_hbm, gs_hbm, gr_hbm, gg_hbm, gw_hbm,
     gx_ref, gz_ref, gb_ref, gc_ref, gs_ref, gr_ref, gg_ref, gw_ref, outs,
     x_ref, z_ref, b_ref, c_ref, step_ref, rate_ref, gain_ref, w_ref, g_ref,
-    gfull, wbuf, dec_src, dec_all, st_send, st_recv, st_pref, st_in,
-    ad_send, ad_recv, ad_pref, ad_in, sq_src, sq_all, cr_src, cr_all,
+    gfull, wbuf, dec_src, dec_all, dec_par, st_send, st_recv, st_pref, st_in,
+    st_other, st_pair, st_half, st_give,
+    ad_send, ad_recv, ad_pref, ad_in, ad_other, ad_pair, ad_half, ad_give, sq_src, sq_all, cr_src, cr_all,
     pt_own, pt_send, pt_recv, rs_o, rs_p, rs_m, buf_p, buf_m, fin,
     tot, t_o, t_p, t_m, tbuf_p, tbuf_m, tfin,
     cpart, crecv, csum, call_, bpart, brecv, bsum, ball,
     gg_src, gg_all, rt_src, rt_all,
     rate_c, lg, lgt, stept, fr, stl, xs2, sc, sct, mix_t, mix_b, ybuf, ycs, gn,
     ubuf, silb, ydb, nb, ntr, ehi, elo, ef2, rprod, colst, ws, qcol, rowp, gxi, mixw, pprod,
-    ins, zs, zr, w1s, w1r, w2s, w2r, wfs, wfr, wds, wdr, des, der, a1s, a1r, a2s, a2r,
+    ins, prs, prr, zs, zr, w1s, w1r, w2s, w2r, wfs, wfr, wds, wdr, des, der, a1s, a1r, a2s, a2r,
     b1s, b1r, b2s, b2r, sqs, sqr, crs, crr, d0s, d0r, r1s, r1r, r2s, r2r,
     c1s, c1r, c2s, c2r, k1s, k1r, k2s, k2r, ggs, ggr, rts, rtr,
 ):
@@ -71,9 +72,6 @@
     p = y * oc + x * c
     rem, div = lax.rem, lax.div
 
-    def at_seq(k):
-        return (div(k, 8), rem(div(k, 2), 4), rem(k, 2), z)
-
     def at_head(k):
         return (y, x, c, k)
 
@@ -106,26 +104,37 @@
         d.start()
         sent.append(d)
 
+    far_first = sorted(
+        ((dy, dx, dc) for dy in range(4) for dx in range(4) for dc in range(2)),
+        key=lambda o: -(min(o[0], 4 - o[0]) + min(o[1], 4 - o[1])) - 0.1 * o[2],
+    )
+    ys, xs, cs = [rem(y + d, 4) for d in range(4)], [rem(x + d, 4) for d in range(4)], (c, oc)
+    peers = [
+        ((ys[dy], xs[dx], cs[dc], z), (ys[dy] * 4 + xs[dx]) * 2 + cs[dc])
+        for dy, dx, dc in far_first
+        if (dy, dx, dc) != (0, 0, 0)
+    ]
+
+    chips = [
+        ((ys[dy], xs[dx], c, z), ys[dy] * 4 + xs[dx])
+        for dy, dx, dc in far_first
+        if dc == 0 and (dy, dx) != (0, 0)
+    ]
+    here = y * 4 + x
+
+    def to_chips(make):
+        for dev, k in chips:
+            make(dev, k).start()
+
     def to_seq(make):
-        def one(d, carry):
-            make(rem(me + d, 32)).start()
-            return carry
-
-        lax.fori_loop(1, 32, one, 0)
+        for dev, k in peers:
+            make(dev, k).start()
 
     def to_head(make):
         for d in (4, 3, 5, 2, 6, 1, 7):
             make(rem(z + d, 8)).start()
 
     barrier = pltpu.get_barrier_semaphore()
-    for d in (4, 3, 5, 2, 6, 1, 7):
-        pl.semaphore_signal(barrier, inc=1, device_id=at_head(rem(z + d, 8)), device_id_type=MESH)
-
-    def greet(d, carry):
-        pl.semaphore_signal(barrier, inc=1, device_id=at_seq(rem(me + d, 32)), device_id_type=MESH)
-        return carry
-
-    lax.fori_loop(1, 32, greet, 0)
     fetches = [
         pltpu.make_async_copy(src, dst, ins.at[i])
         for i, (src, dst) in enumerate((
@@ -135,6 +144,10 @@
     ]
     for f in fetches:
         f.start()
+    for d in (4, 3, 5, 2, 6, 1, 7):
+        pl.semaphore_signal(barrier, inc=1, device_id=at_head(rem(z + d, 8)), device_id_type=MESH)
+    for dev, _ in peers:
+        pl.semaphore_signal(barrier, inc=1, device_id=dev, device_id_type=MESH)
     for f in fetches[:4]:
         f.wait()
 
@@ -183,24 +196,25 @@
     pm, pp, p2 = rem(p + 3, 4), rem(p + 1, 4), rem(p + 2, 4)
     top, low = pl.ds(0, 64), pl.ds(64, 64)
     both_z, both_4 = ((0, 1), (1, 7)), ((0, 1), (1, 3))
-    for k in range(2):
-        rk = pl.ds(128 * k, 128)
+    hc = pl.ds(pl.multiple_of(256 * c, 256), 256)
+    ho = pl.ds(pl.multiple_of(256 * oc, 256), 256)
+
+    def eight(ref, k):
+        return ref.at[pl.ds(pl.multiple_of(8 * k, 8), 8)]
+
+    send(dec_src.at[0], dec_par.at[0], prs.at[4], prr.at[4], partner)
+    send(st_send.at[:, ho], st_other, prs.at[0], prr.at[0], partner)
+    for n in range(2):
         for side, d in both_z:
+            k = n if side == 0 else 1 - n
+            rk = pl.ds(128 * k, 128)
             send(g_ref.at[rk], gfull.at[z, rk], zs.at[side, 0, k], zr.at[side, 0, k], at_head(rem(z + d, 8)))
     for side, d in both_4:
         send(w_ref, wbuf.at[c, p, q], w1s.at[side], w1r.at[side], first(d))
-    to_seq(lambda k: copy(dec_src.at[0], dec_all.at[me], des, der, at_seq(k)))
-
-    def slab(ref, k):
-        return ref.at[
-            pl.ds(pl.multiple_of(8 * div(k, 2), 8), 8),
-            pl.ds(pl.multiple_of(256 * rem(k, 2), 256), 256),
-        ]
-
-    to_seq(lambda k: copy(slab(st_send, k), st_recv.at[me], a1s, a1r, at_seq(k)))
+    to_seq(lambda dev, k: copy(dec_src.at[0], dec_all.at[me], des, der, dev))
+
     for side, d in both_4:
         send(w_ref, wbuf.at[c, p, q], w2s.at[side, 0], w2r.at[side, 0], second(d))
-    st_recv[me] = slab(st_send, me)[...]
     gfull[z] = g_ref[...]
     wbuf[c, p, q] = w_ref[...]
 
@@ -212,6 +226,16 @@
         rs = slice(64 * r, 64 * r + 64)
         sc[rs, :] = jnp.where(iota_i + 64 * r >= iota_j, raw[rs, :], 0.0)
     sct[...] = mm(b_ref[...], ct)
+
+    got(dec_par.at[0], prr.at[4])
+    d_own, d_par = dec_src[0, :, hc], dec_par[0, :, hc]
+    d_0, d_1 = jnp.where(c == 0, d_own, d_par), jnp.where(c == 0, d_par, d_own)
+    got(st_other, prr.at[0])
+    own, other = st_send[:, hc], st_other[...]
+    l_0, l_1 = jnp.where(c == 0, own, other), jnp.where(c == 0, other, own)
+    st_pair[...] = l_1 + d_1 * l_0
+    to_chips(lambda dev, k: copy(eight(st_pair, k), st_recv.at[here], a1s, a1r, dev))
+    st_recv[here] = eight(st_pair, here)[...]
 
     got(wbuf.at[c, p, qm], w1r.at[0])
     send(wbuf.at[c, p, qm, top], wbuf.at[c, p, qm, top], w1s.at[2], w1r.at[2], first(1))
@@ -250,14 +274,13 @@
     def z_block(side, j):
         return rem(z + 8 - j, 8) if side == 0 else rem(z + j, 8)
 
-    def z_forward(j):
-        for k in range(2):
-            rk = pl.ds(128 * k, 128)
-            for side, d in both_z:
-                blk = gfull.at[z_block(side, j), rk]
-                got(blk, zr.at[side, j - 1, k])
-                if j < 3 or k == side:
-                    send(blk, blk, zs.at[side, j, k], zr.at[side, j, k], at_head(rem(z + d, 8)))
+    def z_forward(j, n):
+        for side, d in both_z:
+            k = n if side == 0 else 1 - n
+            blk = gfull.at[z_block(side, j), pl.ds(128 * k, 128)]
+            got(blk, zr.at[side, j - 1, k])
+            if j < 3 or n == 0:
+                send(blk, blk, zs.at[side, j, k], zr.at[side, j, k], at_head(rem(z + d, 8)))
 
     spots = (q, qm, qp, q2, q2)
 
@@ -287,34 +310,48 @@
 
     def scan(recv, pref, back):
         s = jnp.zeros((8, 256), F32)
-        for k in reversed(range(32)) if back else range(32):
+        for k in reversed(range(16)) if back else range(16):
             pref[k] = s
-            s = s * dec_all[k, :, pl.ds(pl.multiple_of(256 * c, 256), 256)] + recv[k]
-
-    many = pl.ds(0, 31)
+            s = s * (dec_all[2 * k, :, hc] * dec_all[2 * k + 1, :, hc]) + recv[k]
+
+    many, few = pl.ds(0, 31), pl.ds(0, 15)
 
     inside(0)
     w_forward(0)
     w_second_of_opposite()
     to_partner(0, p)
     inside(1)
-    z_forward(1)
+    z_forward(1, 0)
+    z_forward(1, 1)
     got(dec_all.at[many], der)
-    got(st_recv.at[many], a1r)
+    got(st_recv.at[few], a1r)
     scan(st_recv, st_pref, False)
-    to_seq(lambda k: copy(st_pref.at[k], slab(st_in, me), a2s, a2r, at_seq(k)))
-    slab(st_in, me)[...] = st_pref[me]
+    to_chips(lambda dev, k: copy(st_pref.at[k], eight(st_half, here), a2s, a2r, dev))
+    eight(st_half, here)[...] = st_pref[here]
     w_forward(1)
     w_forward(2)
     inside(2)
-    inside(3)
     w_forward(3)
     w_forward(4)
     to_partner(1, pm)
     to_partner(2, pp)
-    z_forward(2)
-
-    got(st_recv.at[many], a2r)
+    z_forward(2, 0)
+    inside(3)
+    z_forward(2, 1)
+    z_forward(3, 0)
+    for n in range(4):
+        i1 = (q, qm, qp, q2)[n]
+        got(wbuf.at[c, p2, i1, top], wfr.at[0, n])
+        got(wbuf.at[c, p2, i1, low], wfr.at[1, n])
+    to_partner(3, p2)
+
+    got(st_recv.at[few], a2r)
+    enter = st_half[...]
+    later = d_0 * enter + jnp.where(c == 0, st_send[:, hc], st_other[...])
+    st_give[...] = jnp.where(c == 0, later, enter)
+    send(st_give, st_in.at[:, hc], prs.at[1], prr.at[1], partner)
+    st_in[:, hc] = jnp.where(c == 0, enter, later)
+    got(st_in.at[:, ho], prr.at[1])
     s_hi, s_lo = split2(st_in[...])
     cc = lanes(c_ref[...], c_ref[...])
     gain = gain_ref[...]
@@ -343,12 +380,7 @@
     sq_all[z] = sq
     to_head(lambda k: copy(sq_src.at[0], sq_all.at[z], sqs, sqr, at_head(k)))
 
-    for n in range(4):
-        i1 = (q, qm, qp, q2)[n]
-        got(wbuf.at[c, p2, i1, top], wfr.at[0, n])
-        got(wbuf.at[c, p2, i1, low], wfr.at[1, n])
-    to_partner(3, p2)
-    z_forward(3)
+    z_forward(3, 1)
     for n in range(4):
         got(wbuf.at[oc, p], wdr.at[n])
 
@@ -432,10 +464,9 @@
         rprod[rs, 0:512] = hi
         rprod[rs, 512:1024] = lo
     ad_send[...] = mm(lanes(ct, ct), ef2[...])
-    to_seq(lambda k: copy(slab(ad_send, k), ad_recv.at[me], b1s, b1r, at_seq(k)))
-    ad_recv[me] = slab(ad_send, me)[...]
+    send(ad_send.at[:, ho], ad_other, prs.at[2], prr.at[2], partner)
     store(gz_ref, gz_hbm)
-    to_seq(lambda k: copy(gg_src.at[0], gg_all.at[me], ggs, ggr, at_seq(k)))
+    to_seq(lambda dev, k: copy(gg_src.at[0], gg_all.at[me], ggs, ggr, dev))
 
     got(pt_recv.at[pp], d0r.at[1])
     for i in range(4):
@@ -444,7 +475,6 @@
             pt_own[pp, i] = v
         else:
             rs_p[i] = v.astype(BF)
-    send(rs_p.at[cd], fin.at[0, cd], r1s.at[2], r1r.at[2], second(1))
     got(pt_recv.at[pm], d0r.at[2])
     for i in range(4):
         v = pt_own[pm, i] + pt_recv[pm, i].astype(F32)
@@ -452,6 +482,12 @@
             rs_m[i] = v.astype(BF)
         else:
             pt_own[pm, i] = v
+    got(ad_other, prr.at[2])
+    own, other = ad_send[:, hc], ad_other[...]
+    ad_pair[...] = jnp.where(c == 0, own, other) + d_0 * jnp.where(c == 0, other, own)
+    to_chips(lambda dev, k: copy(eight(ad_pair, k), ad_recv.at[here], b1s, b1r, dev))
+    ad_recv[here] = eight(ad_pair, here)[...]
+    send(rs_p.at[cd], fin.at[0, cd], r1s.at[2], r1r.at[2], second(1))
     send(rs_m.at[ab], fin.at[1, ab], r1s.at[3], r1r.at[3], second(3))
 
     mask_t = (iota_j >= iota_i, iota_j >= iota_i + 64)
@@ -508,10 +544,10 @@
     for hp in range(4):
         inside_back(hp)
 
-    got(ad_recv.at[many], b1r)
+    got(ad_recv.at[few], b1r)
     scan(ad_recv, ad_pref, True)
-    to_seq(lambda k: copy(ad_pref.at[k], slab(ad_in, me), b2s, b2r, at_seq(k)))
-    slab(ad_in, me)[...] = ad_pref[me]
+    to_chips(lambda dev, k: copy(ad_pref.at[k], eight(ad_half, here), b2s, b2r, dev))
+    eight(ad_half, here)[...] = ad_pref[here]
 
     got(buf_p, r1r.at[0])
     for i in range(2):
@@ -539,7 +575,13 @@
     e16 = lanes(e8, e8)
     rstate = nt(e16, rprod[...])
 
-    got(ad_recv.at[many], b2r)
+    got(ad_recv.at[few], b2r)
+    enter = ad_half[...]
+    sooner = jnp.where(c == 0, ad_other[...], ad_send[:, hc]) + d_1 * enter
+    ad_give[...] = jnp.where(c == 0, enter, sooner)
+    send(ad_give, ad_in.at[:, hc], prs.at[3], prr.at[3], partner)
+    ad_in[:, hc] = jnp.where(c == 0, sooner, enter)
+    got(ad_in.at[:, ho], prr.at[3])
     a_hi, a_lo = split2(ad_in[...])
     gk = gk + nt(lanes(xs2[0:256], xs2[256:512], xs2[0:256]), lanes(a_hi, a_hi, a_lo))
     for k in range(8):
@@ -581,7 +623,7 @@
     d1 = lax.broadcasted_iota(jnp.int32, (8, 128), 1)
     rt_src[0] = jnp.sum(jnp.where(d0 == d1, rp, 0.0), axis=0, keepdims=True)
     rt_all[me] = rt_src[0]
-    to_seq(lambda k: copy(rt_src.at[0], rt_all.at[me], rts, rtr, at_seq(k)))
+    to_seq(lambda dev, k: copy(rt_src.at[0], rt_all.at[me], rts, rtr, dev))
     store(gs_ref, gs_hbm)
 
     got(fin.at[0, cd], r1r.at[2])
@@ -647,12 +689,14 @@
         d.wait_send()
     for d in stored:
         d.wait()
-    for ref, sem in (
-        (dec_all, des), (st_recv, a1s), (st_recv, a2s), (ad_recv, b1s), (ad_recv, b2s),
+    for ref, sem in [
+        (dec_all, des),
         (gg_all, ggs), (rt_all, rts),
-    ):
+    ]:
         left(ref.at[many], sem)
-    for ref, sem in ((sq_all, sqs), (cr_all, crs), (crecv, c1s), (call_, c2s), (brecv, k1s), (ball, k2s)):
+    for ref, sem in [(st_recv, a1s), (st_recv, a2s), (ad_recv, b1s), (ad_recv, b2s)]:
+        left(ref.at[few], sem)
+    for ref, sem in [(sq_all, sqs), (cr_all, crs), (crecv, c1s), (call_, c2s), (brecv, k1s), (ball, k2s)]:
         left(ref.at[seven], sem)
 
 
@@ -679,9 +723,11 @@
         V((256, 512), BF), V((256, 512), BF), V((256, 128), BF), V((256, 128), BF),
         V((8, 256), F32), V((1, 8), F32), V((1, 512), F32), V((128, 512), BF), V((256, 512), BF),
         V((8, 256, 512), BF), V((2, 4, 4, 128, 512), BF),
-        V((1, 1, 512), F32), V((32, 1, 512), F32),
-        V((128, 512), F32), V((32, 8, 256), F32), V((32, 8, 256), F32), V((128, 512), F32),
-        V((128, 512), F32), V((32, 8, 256), F32), V((32, 8, 256), F32), V((128, 512), F32),
+        V((1, 1, 512), F32), V((32, 1, 512), F32), V((1, 1, 512), F32),
+        V((128, 512), F32), V((16, 8, 256), F32), V((16, 8, 256), F32), V((128, 512), F32),
+        V((128, 256), F32), V((128, 256), F32), V((128, 256), F32), V((128, 256), F32),
+        V((128, 512), F32), V((16, 8, 256), F32), V((16, 8, 256), F32), V((128, 512), F32),
+        V((128, 256), F32), V((128, 256), F32), V((128, 256), F32), V((128, 256), F32),
         V((1, 1, 256), F32), V((8, 1, 256), F32), V((1, 1, 256), F32), V((8, 1, 256), F32),
         V((4, 4, 512, 128), F32), V((4, 4, 512, 128), BF), V((4, 4, 512, 128), BF),
         V((4, 512, 128), BF), V((4, 512, 128), BF), V((4, 512, 128), BF),
@@ -701,7 +747,7 @@
         V((256, 512), BF), V((256, 512), BF), V((512, 512), BF), V((256, 1024), BF),
         V((256, 128), F32), V((256, 256), F32), V((256, 128), F32), V((8, 256), F32),
         V((256, 512), F32), V((2, 256, 512), BF), V((256, 1024), F32),
-        dma((9,)), dma((2, 4, 2)), dma((2, 4, 2)), dma((4,)), dma((4,)), dma((2, 5)), dma((2, 5)),
+        dma((9,)), dma((5,)), dma((5,)), dma((2, 4, 2)), dma((2, 4, 2)), dma((4,)), dma((4,)), dma((2, 5)), dma((2, 5)),
         dma((2, 4)), dma((2, 4)), dma((4,)), dma((4,)),
         dma, dma, dma, dma, dma, dma, dma, dma, dma, dma, dma, dma, dma, dma,
         dma((4,)), dma((4,)), dma((8,)), dma((8,)), dma((4,)), dma((4,)),

time: 74 us -> 71.5 us (0.966)
  Pallas kernels: 73.2 us -> 70.8 us
    pallas_call x1, Pallas kernels: 71.1 us -> 68.7 us  [on_device(): pl.pallas_call(kernel, out_shape=outs, in_specs=[far] * 9, out_specs=[far...]
where the time goes in v3:
time: 71.5 us; the launch traced here: 71.4 us
  Pallas kernels  70.8 us (99%)
    pallas_call x1, Pallas kernels, on_device(): pl.pallas_call(kernel, out_shape=outs, in_specs=[far] * 9, out_specs=[far...  68.7 us
    pallas_call x1, Pallas kernels, on_device(): pl.pallas_call(hand_over, out_shape=outs, in_specs=[far] * 8, out_specs=[...  2.07 us

profile of v3, /device:TPU:1, one launch (start us, length us, event | category | flops | bytes accessed | tf_op | source)
XLA Modules:
  0.0 71.4 jit_solution(16182618856951908687)
XLA Ops:
  0.6 68.7 %shard_map.152 = (bf16[256,512]{1,0:T(8,128)(2,1)}, bf16[256,512]{1,0:T(8,128)(2,1)}, f32[256,128]{1,0:T(8,128)}, f32[256,128]{1,0:T(8,128)}, f32[8,256]{1,0:T(8...) custom-call(bf16[256,512]{1,0:T(8,128)(2,1)} %x_hbm.1, bf16[256,512]{1,0:T(8,128)(2,1)} %z_hbm.1, ...), custom_call_target="tpu_custom_call" | custom-call | tf_op jit(solution)/shard_map/pallas_call | solution.py:767
  69.4 2.1 %shard_map.153 = (bf16[256,512]{1,0:T(8,128)(2,1)}, bf16[256,512]{1,0:T(8,128)(2,1)}, f32[256,128]{1,0:T(8,128)}, f32[256,128]{1,0:T(8,128)}, f32[8,256]{1,0:T(8...) custom-call(bf16[256,512]{1,0:T(8,128)(2,1)} %get-tuple-element.24.refs_0_, ...), custom_call_target="tpu_custom_call" | custom-call | tf_op jit(solution)/shard_map/pallas_call | solution.py:780

commit v4 on v3

--- a/solution.py
+++ b/solution.py
@@ -49,7 +49,7 @@
     gx_hbm, gz_hbm, gb_hbm, gc_hbm, gs_hbm, gr_hbm, gg_hbm, gw_hbm,
     gx_ref, gz_ref, gb_ref, gc_ref, gs_ref, gr_ref, gg_ref, gw_ref, outs,
     x_ref, z_ref, b_ref, c_ref, step_ref, rate_ref, gain_ref, w_ref, g_ref,
-    gfull, wbuf, dec_src, dec_all, dec_par, st_send, st_recv, st_pref, st_in,
+    gfull, wbuf, dec_src, dec_all, dec_par, dec_two, st_send, st_recv, st_pref, st_in,
     st_other, st_pair, st_half, st_give,
     ad_send, ad_recv, ad_pref, ad_in, ad_other, ad_pair, ad_half, ad_give, sq_src, sq_all, cr_src, cr_all,
     pt_own, pt_send, pt_recv, rs_o, rs_p, rs_m, buf_p, buf_m, fin,
@@ -58,7 +58,7 @@
     gg_src, gg_all, rt_src, rt_all,
     rate_c, lg, lgt, stept, fr, stl, xs2, sc, sct, mix_t, mix_b, ybuf, ycs, gn,
     ubuf, silb, ydb, nb, ntr, ehi, elo, ef2, rprod, colst, ws, qcol, rowp, gxi, mixw, pprod,
-    ins, prs, prr, zs, zr, w1s, w1r, w2s, w2r, wfs, wfr, wds, wdr, des, der, a1s, a1r, a2s, a2r,
+    kx, ky, kyy, kc, kz1, kz2, kz3, ins, prs, prr, zs, zr, w1s, w1r, w2s, w2r, wfs, wfr, wds, wdr, des, der, a1s, a1r, a2s, a2r,
     b1s, b1r, b2s, b2r, sqs, sqr, crs, crr, d0s, d0r, r1s, r1r, r2s, r2r,
     c1s, c1r, c2s, c2r, k1s, k1r, k2s, k2r, ggs, ggr, rts, rtr,
 ):
@@ -134,21 +134,48 @@
         for d in (4, 3, 5, 2, 6, 1, 7):
             make(rem(z + d, 8)).start()
 
+    near_x = [(y, rem(x + d, 4), c, z) for d in (1, 3)]
+    near_y = [(rem(y + d, 4), x, c, z) for d in (1, 3)]
+    near_z = [(y, x, c, rem(z + d, 8)) for d in (1, 7)]
+
+    def tell(sem, devices):
+        for dev in devices:
+            pl.semaphore_signal(sem, inc=1, device_id=dev, device_id_type=MESH)
+
     barrier = pltpu.get_barrier_semaphore()
     fetches = [
         pltpu.make_async_copy(src, dst, ins.at[i])
         for i, (src, dst) in enumerate((
-            (step_hbm, step_ref), (rate_hbm, rate_ref), (gain_hbm, gain_ref), (b_hbm, b_ref),
-            (x_hbm, x_ref), (c_hbm, c_ref), (g_hbm, g_ref), (w_hbm, w_ref), (z_hbm, z_ref),
+            (g_hbm, g_ref), (w_hbm, w_ref), (step_hbm, step_ref), (rate_hbm, rate_ref),
+            (b_hbm, b_ref), (x_hbm, x_ref), (c_hbm, c_ref), (gain_hbm, gain_ref), (z_hbm, z_ref),
         ))
     ]
     for f in fetches:
         f.start()
-    for d in (4, 3, 5, 2, 6, 1, 7):
-        pl.semaphore_signal(barrier, inc=1, device_id=at_head(rem(z + d, 8)), device_id_type=MESH)
-    for dev, _ in peers:
-        pl.semaphore_signal(barrier, inc=1, device_id=dev, device_id_type=MESH)
-    for f in fetches[:4]:
+    tell(barrier, near_z + near_x + near_y + [partner])
+    for f in fetches[:2]:
+        f.wait()
+    pl.semaphore_wait(barrier, 7)
+    tell(kx, near_x)
+    tell(kz1, near_z)
+
+    qm, qp, q2 = rem(q + 3, 4), rem(q + 1, 4), rem(q + 2, 4)
+    pm, pp, p2 = rem(p + 3, 4), rem(p + 1, 4), rem(p + 2, 4)
+    top, low = pl.ds(0, 64), pl.ds(64, 64)
+    both_z, both_4 = ((0, 1), (1, 7)), ((0, 1), (1, 3))
+    for n in range(2):
+        for side, d in both_z:
+            k = n if side == 0 else 1 - n
+            rk = pl.ds(128 * k, 128)
+            send(g_ref.at[rk], gfull.at[z, rk], zs.at[side, 0, k], zr.at[side, 0, k], at_head(rem(z + d, 8)))
+    for side, d in both_4:
+        send(w_ref, wbuf.at[c, p, q], w1s.at[side], w1r.at[side], first(d))
+    for side, d in both_4:
+        send(w_ref, wbuf.at[c, p, q], w2s.at[side, 0], w2r.at[side, 0], second(d))
+    gfull[z] = g_ref[...]
+    wbuf[c, p, q] = w_ref[...]
+
+    for f in fetches[2:5]:
         f.wait()
 
     i8 = lax.broadcasted_iota(jnp.int32, (8, 8), 0)
@@ -178,24 +205,19 @@
     fr[...] = spread_heads(jnp.exp(logs_t))
     stl[...] = spread_heads(step_t * jnp.exp(logs_t[255:256, :] - logs_t))
     dec_src[0] = fr[255:256, :]
-    dec_all[me] = fr[255:256, :]
     bt = b_ref[...].T
-    fetches[4].wait()
+    fetches[5].wait()
+    pl.semaphore_wait(kx, 2)
+    tell(ky, near_y)
     for r in range(4):
         rs = slice(64 * r, 64 * r + 64)
         hi, lo = split2(x_ref[rs, :].astype(F32) * stl[rs, :])
         xs2[rs, :] = hi
         xs2[64 * r + 256 : 64 * r + 320, :] = lo
     st_send[...] = mm(lanes(bt, bt), xs2[...])
-    for f in fetches[5:]:
+    for f in fetches[6:]:
         f.wait()
 
-    pl.semaphore_wait(barrier, 38)
-
-    qm, qp, q2 = rem(q + 3, 4), rem(q + 1, 4), rem(q + 2, 4)
-    pm, pp, p2 = rem(p + 3, 4), rem(p + 1, 4), rem(p + 2, 4)
-    top, low = pl.ds(0, 64), pl.ds(64, 64)
-    both_z, both_4 = ((0, 1), (1, 7)), ((0, 1), (1, 3))
     hc = pl.ds(pl.multiple_of(256 * c, 256), 256)
     ho = pl.ds(pl.multiple_of(256 * oc, 256), 256)
 
@@ -204,20 +226,6 @@
 
     send(dec_src.at[0], dec_par.at[0], prs.at[4], prr.at[4], partner)
     send(st_send.at[:, ho], st_other, prs.at[0], prr.at[0], partner)
-    for n in range(2):
-        for side, d in both_z:
-            k = n if side == 0 else 1 - n
-            rk = pl.ds(128 * k, 128)
-            send(g_ref.at[rk], gfull.at[z, rk], zs.at[side, 0, k], zr.at[side, 0, k], at_head(rem(z + d, 8)))
-    for side, d in both_4:
-        send(w_ref, wbuf.at[c, p, q], w1s.at[side], w1r.at[side], first(d))
-    to_seq(lambda dev, k: copy(dec_src.at[0], dec_all.at[me], des, der, dev))
-
-    for side, d in both_4:
-        send(w_ref, wbuf.at[c, p, q], w2s.at[side, 0], w2r.at[side, 0], second(d))
-    gfull[z] = g_ref[...]
-    wbuf[c, p, q] = w_ref[...]
-
     iota_i = lax.broadcasted_iota(jnp.int32, (64, 256), 0)
     iota_j = lax.broadcasted_iota(jnp.int32, (64, 256), 1)
     ct = c_ref[...].T
@@ -227,6 +235,8 @@
         sc[rs, :] = jnp.where(iota_i + 64 * r >= iota_j, raw[rs, :], 0.0)
     sct[...] = mm(b_ref[...], ct)
 
+    pl.semaphore_wait(ky, 2)
+    tell(kyy, near_y)
     got(dec_par.at[0], prr.at[4])
     d_own, d_par = dec_src[0, :, hc], dec_par[0, :, hc]
     d_0, d_1 = jnp.where(c == 0, d_own, d_par), jnp.where(c == 0, d_par, d_own)
@@ -234,6 +244,11 @@
     own, other = st_send[:, hc], st_other[...]
     l_0, l_1 = jnp.where(c == 0, own, other), jnp.where(c == 0, other, own)
     st_pair[...] = l_1 + d_1 * l_0
+    dec_two[0] = dec_src[0] * dec_par[0]
+    dec_all[here] = dec_two[0]
+    pl.semaphore_wait(kyy, 2)
+    tell(kc, [partner])
+    to_chips(lambda dev, k: copy(dec_two.at[0], dec_all.at[here], des, der, dev))
     to_chips(lambda dev, k: copy(eight(st_pair, k), st_recv.at[here], a1s, a1r, dev))
     st_recv[here] = eight(st_pair, here)[...]
 
@@ -312,7 +327,7 @@
         s = jnp.zeros((8, 256), F32)
         for k in reversed(range(16)) if back else range(16):
             pref[k] = s
-            s = s * (dec_all[2 * k, :, hc] * dec_all[2 * k + 1, :, hc]) + recv[k]
+            s = s * dec_all[k, :, hc] + recv[k]
 
     many, few = pl.ds(0, 31), pl.ds(0, 15)
 
@@ -321,9 +336,11 @@
     w_second_of_opposite()
     to_partner(0, p)
     inside(1)
+    pl.semaphore_wait(kz1, 2)
+    tell(kz2, near_z)
     z_forward(1, 0)
     z_forward(1, 1)
-    got(dec_all.at[many], der)
+    got(dec_all.at[few], der)
     got(st_recv.at[few], a1r)
     scan(st_recv, st_pref, False)
     to_chips(lambda dev, k: copy(st_pref.at[k], eight(st_half, here), a2s, a2r, dev))
@@ -335,6 +352,8 @@
     w_forward(4)
     to_partner(1, pm)
     to_partner(2, pp)
+    pl.semaphore_wait(kz2, 2)
+    tell(kz3, near_z)
     z_forward(2, 0)
     inside(3)
     z_forward(2, 1)
@@ -378,6 +397,7 @@
     sq = jnp.sum(jnp.transpose(pprod[:, 0:128]), axis=0, keepdims=True)
     sq_src[0] = sq
     sq_all[z] = sq
+    pl.semaphore_wait(kz3, 2)
     to_head(lambda k: copy(sq_src.at[0], sq_all.at[z], sqs, sqr, at_head(k)))
 
     z_forward(3, 1)
@@ -466,6 +486,7 @@
     ad_send[...] = mm(lanes(ct, ct), ef2[...])
     send(ad_send.at[:, ho], ad_other, prs.at[2], prr.at[2], partner)
     store(gz_ref, gz_hbm)
+    pl.semaphore_wait(kc, 1)
     to_seq(lambda dev, k: copy(gg_src.at[0], gg_all.at[me], ggs, ggr, dev))
 
     got(pt_recv.at[pp], d0r.at[1])
@@ -690,11 +711,10 @@
     for d in stored:
         d.wait()
     for ref, sem in [
-        (dec_all, des),
         (gg_all, ggs), (rt_all, rts),
     ]:
         left(ref.at[many], sem)
-    for ref, sem in [(st_recv, a1s), (st_recv, a2s), (ad_recv, b1s), (ad_recv, b2s)]:
+    for ref, sem in [(dec_all, des), (st_recv, a1s), (st_recv, a2s), (ad_recv, b1s), (ad_recv, b2s)]:
         left(ref.at[few], sem)
     for ref, sem in [(sq_all, sqs), (cr_all, crs), (crecv, c1s), (call_, c2s), (brecv, k1s), (ball, k2s)]:
         left(ref.at[seven], sem)
@@ -716,14 +736,14 @@
     inputs, gates, b_proj, c_proj, step_size, decay_rate, norm_gain, out_weight, grad_out
 ):
     V = pltpu.VMEM
-    dma = pltpu.SemaphoreType.DMA
+    dma, reg = pltpu.SemaphoreType.DMA, pltpu.SemaphoreType.REGULAR
     scratch = [
         V((256, 512), BF), V((256, 512), BF), V((256, 128), F32), V((256, 128), F32),
         V((8, 256), F32), V((1, 8), F32), V((1, 512), F32), V((128, 512), F32), dma((8,)),
         V((256, 512), BF), V((256, 512), BF), V((256, 128), BF), V((256, 128), BF),
         V((8, 256), F32), V((1, 8), F32), V((1, 512), F32), V((128, 512), BF), V((256, 512), BF),
         V((8, 256, 512), BF), V((2, 4, 4, 128, 512), BF),
-        V((1, 1, 512), F32), V((32, 1, 512), F32), V((1, 1, 512), F32),
+        V((1, 1, 512), F32), V((16, 1, 512), F32), V((1, 1, 512), F32), V((1, 1, 512), F32),
         V((128, 512), F32), V((16, 8, 256), F32), V((16, 8, 256), F32), V((128, 512), F32),
         V((128, 256), F32), V((128, 256), F32), V((128, 256), F32), V((128, 256), F32),
         V((128, 512), F32), V((16, 8, 256), F32), V((16, 8, 256), F32), V((128, 512), F32),
@@ -747,7 +767,7 @@
         V((256, 512), BF), V((256, 512), BF), V((512, 512), BF), V((256, 1024), BF),
         V((256, 128), F32), V((256, 256), F32), V((256, 128), F32), V((8, 256), F32),
         V((256, 512), F32), V((2, 256, 512), BF), V((256, 1024), F32),
-        dma((9,)), dma((5,)), dma((5,)), dma((2, 4, 2)), dma((2, 4, 2)), dma((4,)), dma((4,)), dma((2, 5)), dma((2, 5)),
+        reg, reg, reg, reg, reg, reg, reg, dma((9,)), dma((5,)), dma((5,)), dma((2, 4, 2)), dma((2, 4, 2)), dma((4,)), dma((4,)), dma((2, 5)), dma((2, 5)),
         dma((2, 4)), dma((2, 4)), dma((4,)), dma((4,)),
         dma, dma, dma, dma, dma, dma, dma, dma, dma, dma, dma, dma, dma, dma,
         dma((4,)), dma((4,)), dma((8,)), dma((8,)), dma((4,)), dma((4,)),

time: 71.5 us -> 69.7 us (0.975)
  Pallas kernels: 70.8 us -> 69 us
    pallas_call x1, Pallas kernels: 68.7 us -> 66.9 us  [on_device(): pl.pallas_call(kernel, out_shape=outs, in_specs=[far] * 9, out_specs=[far...]
where the time goes in v4:
time: 69.7 us; the launch traced here: 69.6 us
  Pallas kernels  69 us (99%)
    pallas_call x1, Pallas kernels, on_device(): pl.pallas_call(kernel, out_shape=outs, in_specs=[far] * 9, out_specs=[far...  66.9 us
    pallas_call x1, Pallas kernels, on_device(): pl.pallas_call(hand_over, out_shape=outs, in_specs=[far] * 8, out_specs=[...  2.07 us

profile of v4, /device:TPU:1, one launch (start us, length us, event | category | flops | bytes accessed | tf_op | source)
XLA Modules:
  0.0 69.6 jit_solution(1156871035189100589)
XLA Ops:
  0.6 66.9 %shard_map.152 = (bf16[256,512]{1,0:T(8,128)(2,1)}, bf16[256,512]{1,0:T(8,128)(2,1)}, f32[256,128]{1,0:T(8,128)}, f32[256,128]{1,0:T(8,128)}, f32[8,256]{1,0:T(8...) custom-call(bf16[256,512]{1,0:T(8,128)(2,1)} %x_hbm.1, bf16[256,512]{1,0:T(8,128)(2,1)} %z_hbm.1, ...), custom_call_target="tpu_custom_call" | custom-call | tf_op jit(solution)/shard_map/pallas_call | solution.py:787
  67.6 2.1 %shard_map.153 = (bf16[256,512]{1,0:T(8,128)(2,1)}, bf16[256,512]{1,0:T(8,128)(2,1)}, f32[256,128]{1,0:T(8,128)}, f32[256,128]{1,0:T(8,128)}, f32[8,256]{1,0:T(8...) custom-call(bf16[256,512]{1,0:T(8,128)(2,1)} %get-tuple-element.24.refs_0_, ...), custom_call_target="tpu_custom_call" | custom-call | tf_op jit(solution)/shard_map/pallas_call | solution.py:800

commit v5 on v4

--- a/solution.py
+++ b/solution.py
@@ -235,6 +235,15 @@
         sc[rs, :] = jnp.where(iota_i + 64 * r >= iota_j, raw[rs, :], 0.0)
     sct[...] = mm(b_ref[...], ct)
 
+    got(wbuf.at[c, p, qm], w1r.at[0])
+    send(wbuf.at[c, p, qm, top], wbuf.at[c, p, qm, top], w1s.at[2], w1r.at[2], first(1))
+    for side, d in both_4:
+        send(wbuf.at[c, p, qm], wbuf.at[c, p, qm], w2s.at[side, 1], w2r.at[side, 1], second(d))
+    got(wbuf.at[c, p, qp], w1r.at[1])
+    send(wbuf.at[c, p, qp, low], wbuf.at[c, p, qp, low], w1s.at[3], w1r.at[3], first(3))
+    for side, d in both_4:
+        send(wbuf.at[c, p, qp], wbuf.at[c, p, qp], w2s.at[side, 2], w2r.at[side, 2], second(d))
+
     pl.semaphore_wait(ky, 2)
     tell(kyy, near_y)
     got(dec_par.at[0], prr.at[4])
@@ -251,15 +260,6 @@
     to_chips(lambda dev, k: copy(dec_two.at[0], dec_all.at[here], des, der, dev))
     to_chips(lambda dev, k: copy(eight(st_pair, k), st_recv.at[here], a1s, a1r, dev))
     st_recv[here] = eight(st_pair, here)[...]
-
-    got(wbuf.at[c, p, qm], w1r.at[0])
-    send(wbuf.at[c, p, qm, top], wbuf.at[c, p, qm, top], w1s.at[2], w1r.at[2], first(1))
-    for side, d in both_4:
-        send(wbuf.at[c, p, qm], wbuf.at[c, p, qm], w2s.at[side, 1], w2r.at[side, 1], second(d))
-    got(wbuf.at[c, p, qp], w1r.at[1])
-    send(wbuf.at[c, p, qp, low], wbuf.at[c, p, qp, low], w1s.at[3], w1r.at[3], first(3))
-    for side, d in both_4:
-        send(wbuf.at[c, p, qp], wbuf.at[c, p, qp], w2s.at[side, 2], w2r.at[side, 2], second(d))
 
     half = lax.broadcasted_iota(jnp.int32, (1, 128), 1)
     keep = (
@@ -333,12 +333,12 @@
 
     inside(0)
     w_forward(0)
+    pl.semaphore_wait(kz1, 2)
+    tell(kz2, near_z)
+    z_forward(1, 0)
     w_second_of_opposite()
     to_partner(0, p)
     inside(1)
-    pl.semaphore_wait(kz1, 2)
-    tell(kz2, near_z)
-    z_forward(1, 0)
     z_forward(1, 1)
     got(dec_all.at[few], der)
     got(st_recv.at[few], a1r)
@@ -348,13 +348,13 @@
     w_forward(1)
     w_forward(2)
     inside(2)
+    pl.semaphore_wait(kz2, 2)
+    tell(kz3, near_z)
+    z_forward(2, 0)
     w_forward(3)
     w_forward(4)
     to_partner(1, pm)
     to_partner(2, pp)
-    pl.semaphore_wait(kz2, 2)
-    tell(kz3, near_z)
-    z_forward(2, 0)
     inside(3)
     z_forward(2, 1)
     z_forward(3, 0)
@@ -362,7 +362,8 @@
         i1 = (q, qm, qp, q2)[n]
         got(wbuf.at[c, p2, i1, top], wfr.at[0, n])
         got(wbuf.at[c, p2, i1, low], wfr.at[1, n])
-    to_partner(3, p2)
+        blk = wbuf.at[c, p2, i1]
+        send(blk, blk, wds.at[3 + n], wdr.at[3 + n], partner)
 
     got(st_recv.at[few], a2r)
     enter = st_half[...]
@@ -401,8 +402,10 @@
     to_head(lambda k: copy(sq_src.at[0], sq_all.at[z], sqs, sqr, at_head(k)))
 
     z_forward(3, 1)
+    for n in range(3):
+        got(wbuf.at[oc, p], wdr.at[n])
     for n in range(4):
-        got(wbuf.at[oc, p], wdr.at[n])
+        got(wbuf.at[oc, p, q], wdr.at[3 + n])
 
     gn[...] = jnp.zeros((256, 512), F32)
 
@@ -486,9 +489,6 @@
     ad_send[...] = mm(lanes(ct, ct), ef2[...])
     send(ad_send.at[:, ho], ad_other, prs.at[2], prr.at[2], partner)
     store(gz_ref, gz_hbm)
-    pl.semaphore_wait(kc, 1)
-    to_seq(lambda dev, k: copy(gg_src.at[0], gg_all.at[me], ggs, ggr, dev))
-
     got(pt_recv.at[pp], d0r.at[1])
     for i in range(4):
         v = pt_own[pp, i] + pt_recv[pp, i].astype(F32)
@@ -508,6 +508,8 @@
     ad_pair[...] = jnp.where(c == 0, own, other) + d_0 * jnp.where(c == 0, other, own)
     to_chips(lambda dev, k: copy(eight(ad_pair, k), ad_recv.at[here], b1s, b1r, dev))
     ad_recv[here] = eight(ad_pair, here)[...]
+    pl.semaphore_wait(kc, 1)
+    to_seq(lambda dev, k: copy(gg_src.at[0], gg_all.at[me], ggs, ggr, dev))
     send(rs_p.at[cd], fin.at[0, cd], r1s.at[2], r1r.at[2], second(1))
     send(rs_m.at[ab], fin.at[1, ab], r1s.at[3], r1r.at[3], second(3))
 
@@ -768,7 +770,7 @@
         V((256, 128), F32), V((256, 256), F32), V((256, 128), F32), V((8, 256), F32),
         V((256, 512), F32), V((2, 256, 512), BF), V((256, 1024), F32),
         reg, reg, reg, reg, reg, reg, reg, dma((9,)), dma((5,)), dma((5,)), dma((2, 4, 2)), dma((2, 4, 2)), dma((4,)), dma((4,)), dma((2, 5)), dma((2, 5)),
-        dma((2, 4)), dma((2, 4)), dma((4,)), dma((4,)),
+        dma((2, 4)), dma((2, 4)), dma((7,)), dma((7,)),
         dma, dma, dma, dma, dma, dma, dma, dma, dma, dma, dma, dma, dma, dma,
         dma((4,)), dma((4,)), dma((8,)), dma((8,)), dma((4,)), dma((4,)),
         dma, dma, dma, dma, dma, dma, dma, dma, dma, dma, dma, dma,

time: 69.7 us -> 66.9 us (0.960)
  Pallas kernels: 69 us -> 66.2 us
    pallas_call x1, Pallas kernels: 66.9 us -> 64.1 us  [on_device(): pl.pallas_call(kernel, out_shape=outs, in_specs=[far] * 9, out_specs=[far...]
where the time goes in v5:
time: 66.9 us; the launch traced here: 66.8 us
  Pallas kernels  66.2 us (99%)
    pallas_call x1, Pallas kernels, on_device(): pl.pallas_call(kernel, out_shape=outs, in_specs=[far] * 9, out_specs=[far...  64.1 us
    pallas_call x1, Pallas kernels, on_device(): pl.pallas_call(hand_over, out_shape=outs, in_specs=[far] * 8, out_specs=[...  2.07 us

profile of v5, /device:TPU:1, one launch (start us, length us, event | category | flops | bytes accessed | tf_op | source)
XLA Modules:
  0.0 66.8 jit_solution(3115397454440061996)
XLA Ops:
  0.6 64.1 %shard_map.152 = (bf16[256,512]{1,0:T(8,128)(2,1)}, bf16[256,512]{1,0:T(8,128)(2,1)}, f32[256,128]{1,0:T(8,128)}, f32[256,128]{1,0:T(8,128)}, f32[8,256]{1,0:T(8...) custom-call(bf16[256,512]{1,0:T(8,128)(2,1)} %x_hbm.1, bf16[256,512]{1,0:T(8,128)(2,1)} %z_hbm.1, ...), custom_call_target="tpu_custom_call" | custom-call | tf_op jit(solution)/shard_map/pallas_call | solution.py:789
  64.7 2.1 %shard_map.153 = (bf16[256,512]{1,0:T(8,128)(2,1)}, bf16[256,512]{1,0:T(8,128)(2,1)}, f32[256,128]{1,0:T(8,128)}, f32[256,128]{1,0:T(8,128)}, f32[8,256]{1,0:T(8...) custom-call(bf16[256,512]{1,0:T(8,128)(2,1)} %get-tuple-element.24.refs_0_, ...), custom_call_target="tpu_custom_call" | custom-call | tf_op jit(solution)/shard_map/pallas_call | solution.py:802

commit v6 on v5

--- a/solution.py
+++ b/solution.py
@@ -567,20 +567,6 @@
     for hp in range(4):
         inside_back(hp)
 
-    got(ad_recv.at[few], b1r)
-    scan(ad_recv, ad_pref, True)
-    to_chips(lambda dev, k: copy(ad_pref.at[k], eight(ad_half, here), b2s, b2r, dev))
-    eight(ad_half, here)[...] = ad_pref[here]
-
-    got(buf_p, r1r.at[0])
-    for i in range(2):
-        rs_p[i] = (pt_own[pp, i] + buf_p[i].astype(F32)).astype(BF)
-    send(rs_p.at[ab], fin.at[0, ab], r2s.at[0], r2r.at[0], second(1))
-    got(buf_m, r1r.at[1])
-    for i in range(2):
-        rs_m[2 + i] = (pt_own[pm, 2 + i] + buf_m[i].astype(F32)).astype(BF)
-    send(rs_m.at[cd], fin.at[1, cd], r2s.at[1], r2r.at[1], second(3))
-
     ws[128:256, 0:128] = jnp.zeros((128, 128), F32)
     w_hi, w_lo = split2(jnp.transpose(ws[...]))
     gq = mm(lanes(w_hi, w_lo), rows(b_ref[...], b_ref[...]))
@@ -591,6 +577,20 @@
     to_head(lambda k: copy(cpart.at[k], crecv.at[z], c1s, c1r, at_head(k)))
     w_hi, w_lo = split2(ws[...])
     gk = mm(lanes(w_hi, w_lo), rows(c_ref[...], c_ref[...]))
+
+    got(ad_recv.at[few], b1r)
+    scan(ad_recv, ad_pref, True)
+    to_chips(lambda dev, k: copy(ad_pref.at[k], eight(ad_half, here), b2s, b2r, dev))
+    eight(ad_half, here)[...] = ad_pref[here]
+
+    got(buf_p, r1r.at[0])
+    for i in range(2):
+        rs_p[i] = (pt_own[pp, i] + buf_p[i].astype(F32)).astype(BF)
+    send(rs_p.at[ab], fin.at[0, ab], r2s.at[0], r2r.at[0], second(1))
+    got(buf_m, r1r.at[1])
+    for i in range(2):
+        rs_m[2 + i] = (pt_own[pm, 2 + i] + buf_m[i].astype(F32)).astype(BF)
+    send(rs_m.at[cd], fin.at[1, cd], r2s.at[1], r2r.at[1], second(3))
 
     got(pt_recv.at[p], d0r.at[3])
     for i in range(4):

time: 66.9 us -> 66.9 us (level)
  no operation moved by 1% of the time
where the time goes in v6:
time: 66.9 us; the launch traced here: 66.8 us
  Pallas kernels  66.2 us (99%)
    pallas_call x1, Pallas kernels, on_device(): pl.pallas_call(kernel, out_shape=outs, in_specs=[far] * 9, out_specs=[far...  64.1 us
    pallas_call x1, Pallas kernels, on_device(): pl.pallas_call(hand_over, out_shape=outs, in_specs=[far] * 8, out_specs=[...  2.07 us

profile of v6, /device:TPU:1, one launch (start us, length us, event | category | flops | bytes accessed | tf_op | source)
XLA Modules:
  0.0 66.8 jit_solution(8036086640342483252)
XLA Ops:
  0.6 64.1 %shard_map.152 = (bf16[256,512]{1,0:T(8,128)(2,1)}, bf16[256,512]{1,0:T(8,128)(2,1)}, f32[256,128]{1,0:T(8,128)}, f32[256,128]{1,0:T(8,128)}, f32[8,256]{1,0:T(8...) custom-call(bf16[256,512]{1,0:T(8,128)(2,1)} %x_hbm.1, bf16[256,512]{1,0:T(8,128)(2,1)} %z_hbm.1, ...), custom_call_target="tpu_custom_call" | custom-call | tf_op jit(solution)/shard_map/pallas_call | solution.py:789
  64.7 2.1 %shard_map.153 = (bf16[256,512]{1,0:T(8,128)(2,1)}, bf16[256,512]{1,0:T(8,128)(2,1)}, f32[256,128]{1,0:T(8,128)}, f32[256,128]{1,0:T(8,128)}, f32[8,256]{1,0:T(8...) custom-call(bf16[256,512]{1,0:T(8,128)(2,1)} %get-tuple-element.24.refs_0_, ...), custom_call_target="tpu_custom_call" | custom-call | tf_op jit(solution)/shard_map/pallas_call | solution.py:802
